TPU v7x, 256 devices: a whole 4x4x8 slice. The times are simulated.
256 devices in a mesh: tm: 128 (over x, y, z), rep: 2 (over core).
Axes of the slice: x: 4, y: 4, z: 8, core: 2. Of those that a mesh axis runs over, the one named last changes fastest.
Arguments:
- rows: float32 [524288, 256], P('tm', 'rep'), may hold values from -90 to 90, as said below
- row_mask: int32 [524288], P('tm'), may hold values from 0 to 1, as said below
- key_bucket: int32 [524288], P('tm'), may hold values from 0 to 127
- gain: float32 [256], P('rep'), may hold values from 0.1 to 1.9
Outputs:
- keyed: float32 [393216, 256], P('tm', 'rep')
Inputs may be any that keep to these rules, and one draw needn't show every extreme that they name: `rows`: scale per column differs; entries stay in the range. `row_mask`: of the 4096 rows of each index of tm, at least 2048 pass. Among the passing rows of one index of tm, no key bucket occurs more than 24 times, and one bucket, the same for all indices, occurs exactly 24 times on every index.
All inputs are finite; a program needn't handle non-finite values.
Results may differ from a plain program's by a relative error of at most 0.0003.
Values sent between devices are 32-bit elements; how exact they have to be, the bound alone decides.
A program may use at most 64 MiB of HBM per device.

v0:
```python
import jax
import jax.numpy as jnp
from jax import lax
from jax.sharding import PartitionSpec as P

F = 256
WINDOW = 512


epsilon = 1e-06


def passed_along(x, axis, by):
    devices = lax.axis_size(axis)
    return lax.ppermute(x, axis, [(i, (i + by) % devices) for i in range(devices)])


def sent_to_all(x, axis):
    devices = lax.axis_size(axis)
    return lax.all_to_all(jnp.broadcast_to(x[None], (devices, *x.shape)), axis, 0, 0, tiled=True)


def taken_together(x, axis):
    return sent_to_all(x, axis).sum(axis=0)


def window_sums(extended, width):
    blocks = extended.reshape(-1, width, extended.shape[1])
    steps = jnp.arange(width, dtype=jnp.int32)
    lower = (steps[:, None] >= steps[None, :]).astype(jnp.float32)
    inner = jnp.einsum("ij,bjf->bif", lower, blocks, precision=lax.Precision.HIGHEST)
    totals = inner[:, -1:, :]
    result = inner[1:] + totals[:-1] - inner[:-1]
    return result.reshape(-1, extended.shape[1])


def bucket_ranks(hits):
    size_rows, buckets = hits.shape
    block = min(512, size_rows)
    grouped = hits.reshape(size_rows // block, block, buckets)
    steps = jnp.arange(block, dtype=jnp.int32)
    lower = (steps[:, None] >= steps[None, :]).astype(jnp.float32)
    within = jnp.einsum("ij,bjc->bic", lower, grouped, precision=lax.Precision.HIGHEST)
    totals = within[:, -1, :]
    earlier = jnp.cumsum(totals, axis=0) - totals
    running = (within + earlier[:, None, :]).reshape(size_rows, buckets)
    local_rank = (jnp.sum(running * hits, axis=1) - 1.0).astype(jnp.int32)
    counts = jnp.sum(totals, axis=0).astype(jnp.int32)
    return (local_rank, counts)


def compact_rows(payload, row_mask):
    size_rows, width = payload.shape
    live = row_mask == 1
    order_rank = jnp.cumsum(row_mask) - 1
    target = jnp.where(live, order_rank, size_rows)
    return jnp.zeros((size_rows, width), jnp.float32).at[target].set(payload, mode="drop")


def fill_slots(values, slot, slots_total):
    width = values.shape[1]
    return jnp.zeros((slots_total, width), jnp.float32).at[slot].set(values, mode="drop")


def local(rows, row_mask, key_bucket, gain):
    size_rows, half = rows.shape
    nodes = lax.axis_size("tm")
    most = 3 * size_rows // (4 * nodes)
    positions = jnp.arange(size_rows, dtype=jnp.int32)
    bucket_ids = jnp.arange(nodes, dtype=jnp.int32)
    count = jnp.sum(row_mask)
    own_hits = (key_bucket[:, None] == bucket_ids[None, :]).astype(jnp.float32)
    payload = jnp.concatenate([rows, own_hits], axis=1)
    packed = compact_rows(payload, row_mask)
    compact = packed[:, :half]
    hits = packed[:, half:]
    valid = positions < count
    key_value = jnp.dot(
        hits,
        bucket_ids.astype(jnp.float32),
        precision=lax.Precision.HIGHEST,
        preferred_element_type=jnp.float32,
    )
    compact_key = jnp.where(valid, key_value.astype(jnp.int32), nodes)
    tail = lax.dynamic_slice_in_dim(compact, count - WINDOW, WINDOW, 0)
    earlier_tail = passed_along(tail, "tm", 1)
    extended = jnp.concatenate([earlier_tail, compact], axis=0)
    sums = window_sums(extended, WINDOW)
    local_rank, counts = bucket_ranks(hits)
    slot = jnp.where(valid, compact_key * most + local_rank, nodes * most)
    outgoing = fill_slots(sums, slot, nodes * most)
    outgoing = outgoing.reshape(nodes, most * half)
    sideband = counts.astype(jnp.float32)[:, None]
    received, got_side = (
        lax.all_to_all(outgoing, "tm", split_axis=0, concat_axis=0, tiled=True),
        lax.all_to_all(sideband, "tm", split_axis=0, concat_axis=0, tiled=True),
    )
    got_numbers = got_side.astype(jnp.int32)
    got_starts = jnp.cumsum(got_numbers, axis=0) - got_numbers
    capacity = nodes * most
    start_list = got_starts.reshape(-1)
    spots = jnp.arange(capacity, dtype=jnp.int32)
    sender = jnp.sum((start_list[None, :] <= spots[:, None]).astype(jnp.int32), axis=1) - 1
    sender = jnp.maximum(sender, 0)
    offset = spots - start_list[sender]
    inside = (offset >= 0) & (offset < most)
    lookup = sender * most + jnp.clip(offset, 0, most - 1)
    flat = received.reshape(-1, half)
    keyed = jnp.where(inside[:, None], flat[lookup], jnp.float32(0.0))
    kept = jnp.sum(keyed * keyed, axis=1)
    total_sq = taken_together(kept, "rep")
    keyed = keyed * gain[None, :] / jnp.sqrt(total_sq[:, None] / F + epsilon)
    return keyed


def solution(mesh):
    in_specs = (P("tm", "rep"), P("tm"), P("tm"), P("rep"))
    out_specs = P("tm", "rep")
    return jax.shard_map(local, mesh=mesh, in_specs=in_specs, out_specs=out_specs, check_vma=False)
```

profile of v0, /device:TPU:1, one launch (start us, length us, event | category | flops | bytes accessed | tf_op | source)
XLA Modules:
  0.0 158.7 jit_solution(15269557605474027305)
XLA Ops:
  0.0 1.0 reduce-window.14
  1.0 0.1 slice.39
  1.1 0.1 reduce-window.18
  1.1 0.1 slice_reduce_fusion.2
  1.2 1.4 fusion.21
  2.7 1.3 fusion.6
  4.0 20.2 %scatter_custom_fusion = f32[4096,256]{1,0:T(8,128)} fusion(s32[4096]{0:T(1024)S(1)} %get-tuple-element.8, f32[4096,128]{1,0:T(8,128)S(1)} %fusion.6, f32[]{:T(128)} %constant.57, f32[4096,128]{1,0:T(8,128)} %param.4, f32[]{:T(128)} %constant.14.clone.1), kind=kCustom, calls=%fused_computation.4 | custom fusion | flops 1048576 | bytes 8388616 | tf_op jit(solution)/shard_map/scatter | solution.py:57
  24.2 0.0 slice-start
  24.2 1.6 %slice-done = f32[4096,128]{1,0:T(8,128)S(1)} async-done(((f32[4096,256]{1,0:T(8,128)}), f32[4096,128]{1,0:T(8,128)S(1)}, s32[]{:S(2)}) %slice-start) | async-done | bytes 2097176 | tf_op jit(solution)/shard_map/slice | solution.py:76
  25.8 3.4 %convolution_bitcast_fusion.1 = f32[8,512,128]{1,2,0:T(8,128)S(1)} fusion(f32[8,512,128]{2,1,0:T(8,128)S(1)} %bitcast.37), kind=kOutput, calls=%fused_computation.17 | convolution fusion | flops 3221487616 | bytes 4194304 | tf_op jit(solution)/shard_map/ij,bjc->bic/dot_general | solution.py:43
  29.2 0.0 copy-start
  29.2 1.3 copy-done
  30.6 0.3 slice_reduce_fusion.1
  30.8 0.7 copy.33
  31.6 16.3 %all-to-all-start = ((f32[128,1,1]{2,1,0:T(1,128)}), f32[128,1,1]{2,1,0:T(1,128)S(1)}, u32[]{:S(2)}, u32[]{:S(2)}) async-start(f32[128,1,1]{2,1,0:T(1,128)} %copy.33), calls=%async_computation | async-start | bytes 131072 | tf_op jit(solution)/shard_map/all_to_all | solution.py:96
  47.9 2.1 %fusion.22 = f32[8,128]{1,0:T(8,128)S(1)} fusion(f32[8,512,128]{1,2,0:T(8,128)} %copy-done), kind=kOutput, calls=%fused_computation.54 | output fusion | flops 8192 | bytes 528384 | tf_op jit(solution)/shard_map/jit(cumsum)/reduce_window_sum | solution.py:45
  51.3 1.8 %broadcast_add_fusion = f32[8,512,128]{1,2,0:T(8,128)S(1)} fusion(f32[8,512,128]{1,2,0:T(8,128)} %copy-done, f32[8,128]{1,0:T(8,128)S(1)} %fusion.22), kind=kLoop, calls=%fused_computation.23 | loop fusion | flops 524288 | bytes 4198400 | tf_op jit(solution)/shard_map/add | solution.py:46
  53.1 1.9 %copy.35 = f32[8,512,128]{2,1,0:T(8,128)} copy(f32[8,512,128]{1,2,0:T(8,128)S(1)} %broadcast_add_fusion) | data formatting | bytes 4194304 | tf_op jit(solution)/shard_map/add | solution.py:46
  55.0 3.5 %fusion.20 = (f32[4096,128]{1,0:T(8,128)S(1)}, f32[4096]{0:T(1024)S(1)}) fusion(f32[4096,256]{1,0:T(8,128)} %scatter_custom_fusion, f32[8,512,128]{2,1,0:T(8,128)} %copy.35), kind=kLoop, calls=%fused_computation.52 | loop fusion | flops 1044480 | bytes 8404992 | tf_op jit(solution)/shard_map/slice | solution.py:75
  58.5 0.8 collective-permute-start
  59.4 3.4 %fusion.15 = f32[1,4096]{1,0:T(1,128)S(1)} fusion(f32[4096,256]{1,0:T(8,128)} %scatter_custom_fusion), kind=kOutput, calls=%fused_computation.44 | convolution fusion | flops 6291584 | bytes 2113536 | tf_op jit(solution)/shard_map/dot_general | solution.py:78
  62.8 0.7 compare_select_fusion.1
  63.5 7.7 %collective-permute-done = f32[512,128]{1,0:T(8,128)S(1)} collective-permute-done((f32[512,128]{1,0:T(8,128)S(1)}, f32[512,128]{1,0:T(8,128)S(1)}, u32[]{:S(2)}, u32[]{:S(2)}) %collective-permute-start) | collective-permute-done | bytes 262176 | tf_op jit(solution)/shard_map/ppermute | solution.py:15
  71.1 0.2 pad_maximum_fusion
  71.3 3.9 %convolution_bitcast_fusion = f32[9,512,128]{1,2,0:T(8,128)S(1)} fusion(f32[9,512,128]{2,1,0:T(8,128)S(1)} %bitcast.38), kind=kOutput, calls=%fused_computation.16 | convolution fusion | flops 3624140800 | bytes 4718592 | tf_op jit(solution)/shard_map/ij,bjf->bif/dot_general | solution.py:31
  75.2 0.4 slice_reduce_fusion
  75.6 0.2 slice_subtract_fusion
  75.9 1.9 %copy.37 = f32[8,512,128]{2,1,0:T(8,128)} copy(f32[8,512,128]{1,2,0:T(8,128)S(1)} %slice_subtract_fusion) | data formatting | bytes 4194304 | tf_op jit(solution)/shard_map/sub | solution.py:33
  77.7 12.1 %scatter_custom_fusion.1 = f32[3072,128]{1,0:T(8,128)} fusion(s32[4096]{0:T(1024)S(1)} %compare_select_fusion.1, f32[4096,128]{1,0:T(8,128)} %bitcast.39, f32[]{:T(128)} %constant.14.clone.1), kind=kCustom, calls=%fused_computation.26 | custom fusion | bytes 1573376 | tf_op jit(solution)/shard_map/scatter | solution.py:62
  89.9 0.0 all-to-all-done
  89.9 9.0 %all-to-all-start.1 = ((f32[128,1,3072]{2,1,0:T(1,128)}), f32[128,1,3072]{2,1,0:T(1,128)S(1)}, u32[]{:S(2)}, u32[]{:S(2)}) async-start(f32[128,1,3072]{2,1,0:T(1,128)} %bitcast.13), calls=%async_computation.1 | async-start | bytes 3145728 | tf_op jit(solution)/shard_map/all_to_all | solution.py:95
  98.9 0.2 reduce-window.19
  99.1 0.1 reduce.3
  99.2 2.4 %convert_reduce_fusion.1 = s32[128]{0:T(128)S(1)} fusion(f32[128,1,1]{2,1,0:T(1,128)S(1)} %all-to-all-done), kind=kLoop, calls=%fused_computation.50 | loop fusion | flops 128 | bytes 1024 | tf_op jit(solution)/shard_map/convert_element_type | solution.py:98
  101.5 0.5 convert_reduce_fusion
  102.1 18.7 %gather_fusion = s32[3072]{0:T(1024)S(1)} fusion(s32[128]{0:T(128)S(1)} %sub.50, s32[3072]{0:T(1024)S(1)} %get-tuple-element.9), kind=kCustom, calls=%fused_computation | custom fusion | bytes 36864 | tf_op jit(solution)/shard_map/gather | solution.py:105
  120.8 17.8 %all-to-all-done.1 = f32[128,1,3072]{2,1,0:T(1,128)S(1)} async-done(((f32[128,1,3072]{2,1,0:T(1,128)}), f32[128,1,3072]{2,1,0:T(1,128)S(1)}, u32[]{:S(2)}, u32[]{:S(2)}) %all-to-all-start.1) | async-done | bytes 1572896 | tf_op jit(solution)/shard_map/all_to_all | solution.py:95
  138.6 0.0 copy-start.1
  138.6 8.1 %gather_fusion.1 = f32[3072,128]{1,0:T(8,128)S(1)} fusion(f32[3072,128]{1,0:T(8,128)S(1)} %bitcast.36, s32[3072]{0:T(1024)S(1)} %broadcast_clamp_fusion), kind=kCustom, calls=%fused_computation.1 | custom fusion | bytes 3158016 | tf_op jit(solution)/shard_map/gather | solution.py:109
  146.8 2.1 %multiply_reduce_fusion = f32[3072]{0:T(1024)S(1)} fusion(f32[3072,128]{1,0:T(8,128)S(1)} %gather_fusion.1, pred[3072]{0:T(1024)(128)(4,1)S(1)} %compare_and_fusion), kind=kLoop, calls=%fused_computation.18 | loop fusion | flops 1176576 | bytes 1588224 | tf_op jit(solution)/shard_map/reduce_sum | solution.py:110
  148.9 7.5 %all_to_all.21 = f32[2,1,3072]{2,1,0:T(1,128)S(1)} all-to-all(f32[2,1,3072]{2,1,0:T(1,128)S(1)} %broadcast_in_dim.60), channel_id=1, replica_groups=mesh['tm'=128,'rep'=2] {'rep'}, dimensions={0} | all-to-all | bytes 49152 | tf_op jit(solution)/shard_map/all_to_all | solution.py:20
  156.4 0.0 copy-done.1
  156.4 2.3 %multiply_divide_fusion = f32[3072,128]{1,0:T(8,128)} fusion(f32[3072,128]{1,0:T(8,128)S(1)} %gather_fusion.1, f32[3072]{0:T(1024)S(1)} %add_sqrt_fusion, f32[128]{0:T(128)S(1)} %copy-done.1, pred[3072]{0:T(1024)(128)(4,1)S(1)} %compare_and_fusion), kind=kLoop, calls=%fused_computation.19 | loop fusion | flops 1179648 | bytes 3161600 | tf_op jit(solution)/shard_map/div | solution.py:112
  (11 shorter events, 0.2 us)
Async XLA Ops:
  24.2 1.6 %slice-start = ((f32[4096,256]{1,0:T(8,128)}), f32[4096,128]{1,0:T(8,128)S(1)}, s32[]{:S(2)}) async-start(f32[4096,256]{1,0:T(8,128)} %scatter_custom_fusion), calls=%async_computation.3 | async-start | bytes 4194304 | tf_op jit(solution)/shard_map/slice | solution.py:76
  29.2 1.3 copy-start
  31.6 58.3 %all-to-all-start = ((f32[128,1,1]{2,1,0:T(1,128)}), f32[128,1,1]{2,1,0:T(1,128)S(1)}, u32[]{:S(2)}, u32[]{:S(2)}) async-start(f32[128,1,1]{2,1,0:T(1,128)} %copy.33), calls=%async_computation | async-start | bytes 131072 | tf_op jit(solution)/shard_map/all_to_all | solution.py:96
  58.5 12.6 %collective-permute-start = (f32[512,128]{1,0:T(8,128)S(1)}, f32[512,128]{1,0:T(8,128)S(1)}, u32[]{:S(2)}, u32[]{:S(2)}) collective-permute-start(f32[512,128]{1,0:T(8,128)S(1)} %constant_dynamic-slice_fusion), channel_id=1, source_target_pairs={{0,2},{2,4},{4,6},{6,8},{8,10},{10,12},{12,14},{14,16},{16,18},{18... | collective-permute-start | bytes 786440 | tf_op jit(solution)/shard_map/ppermute | solution.py:15
  89.9 48.8 %all-to-all-start.1 = ((f32[128,1,3072]{2,1,0:T(1,128)}), f32[128,1,3072]{2,1,0:T(1,128)S(1)}, u32[]{:S(2)}, u32[]{:S(2)}) async-start(f32[128,1,3072]{2,1,0:T(1,128)} %bitcast.13), calls=%async_computation.1 | async-start | bytes 3145728 | tf_op jit(solution)/shard_map/all_to_all | solution.py:95
  138.6 17.8 %copy-start.1 = (f32[128]{0:T(128)S(1)}, f32[128]{0:T(128)}, u32[]{:S(2)}) copy-start(f32[128]{0:T(128)} %param.7) | copy-start | bytes 1540
where the time goes:
time: 159 us
  local copies, waits for them, and re-layouts  46.9 us (29%)
  other arithmetic  40.4 us (25%)
  starting transfers between devices  26.1 us (16%)
  waiting for transfers between devices  25.5 us (16%)
  matrix products  10.8 us (7%)
  blocking collectives  7.48 us (5%)
    scatter x1, other arithmetic, compact_rows(): jnp.zeros((size_rows, width), jnp.float32).at[target]  20.2 us
    gather x1, local copies, waits for them, and re-layouts, local(): offset = spots - start_list[sender]  18.7 us
    all_to_all x1, waiting for transfers between devices, local(): lax.all_to_all(outgoing, 'tm', split_axis=0, concat_axis=0, tiled=True)  17.8 us
    all_to_all x1, starting transfers between devices, local(): lax.all_to_all(sideband, 'tm', split_axis=0, concat_axis=0, tiled=True)  16.3 us
    scatter x1, local copies, waits for them, and re-layouts, fill_slots(): jnp.zeros((slots_total, width), jnp.float32).at[slot]  12.1 us
    all_to_all x1, starting transfers between devices, local(): lax.all_to_all(outgoing, 'tm', split_axis=0, concat_axis=0, tiled=True)  8.97 us
    gather x1, local copies, waits for them, and re-layouts, local(): keyed = jnp.where(inside[:, None], flat[lookup], jnp.float32(0.0))  8.11 us
    ppermute x1, waiting for transfers between devices, passed_along(): lax.ppermute(x, axis, [(i, (i + by) % devices) for i in range(devices)])  7.65 us
  transfers between devices with their start and end apart: 3, of which 2 were waited for; matrix products, arithmetic and copies ran while one was open for 34% of the time, Pallas kernels for 0%

commit v1 on v0

v1 whole, which is shorter than its diff:
```python
import functools

import jax
import jax.numpy as jnp
from jax import lax
from jax.experimental import pallas as pl
from jax.experimental.pallas import tpu as pltpu
from jax.sharding import PartitionSpec as P

F = 256
WINDOW = 512
LANES = 128
EPSILON = 1e-06
MESH = pl.DeviceIdType.MESH

BIAS = 32768
INSIDE = WINDOW - BIAS
NOT_LIVE = 16384
EMPTY_SLOT = 16384
EMPTY = 1e9
LIMIT = 1e8


def iota(shape, dim):
    return lax.broadcasted_iota(jnp.int32, shape, dim)


def as_bf16(test):
    return jnp.where(test, jnp.float32(1.0), jnp.float32(0.0)).astype(jnp.bfloat16)


def ones_where(test):
    return jnp.where(test, jnp.bfloat16(1.0), jnp.bfloat16(0.0))


def mm(a, b):
    return jnp.dot(a, b, preferred_element_type=jnp.float32)


def index_kernel(most, rows_ref, mask_ref, key_ref, tail_ref, xcat_ref, crow_ref, cs_ref, empty_ref, x_ref, hits_ref, picks_ref, sem):
    size_rows = rows_ref.shape[0]
    chunks = size_rows // LANES
    load = pltpu.make_async_copy(rows_ref, x_ref, sem)
    load.start()
    mask = mask_ref[...]
    live = mask == 1
    mask_bf = mask.astype(jnp.float32).astype(jnp.bfloat16)
    upper = as_bf16(iota((LANES, LANES), 0) <= iota((LANES, LANES), 1))
    within = mm(mask_bf, upper)
    totals = mm(mask_bf, jnp.ones((LANES, LANES), jnp.bfloat16))
    below = as_bf16(iota((chunks, chunks), 1) < iota((chunks, chunks), 0))
    before = mm(below, totals.astype(jnp.bfloat16))
    count = (before + totals)[chunks - 1 : chunks, :].astype(jnp.int32)
    c = (within + before - 1.0).astype(jnp.int32)
    marked = jnp.where(live, c, NOT_LIVE)
    for a in range(chunks):
        crow_ref[a] = jnp.broadcast_to(marked[a : a + 1, :], (16, LANES)).astype(jnp.int16)
    key = jnp.where(live, key_ref[...], -1)
    buckets = iota((LANES, LANES), 0)
    for a in range(chunks):
        hits_ref[:, a * LANES : (a + 1) * LANES] = as_bf16(jnp.broadcast_to(key[a : a + 1, :], (LANES, LANES)) == buckets)
    upper2 = as_bf16(iota((256, 256), 0) <= iota((256, 256), 1))
    carry = jnp.zeros((LANES, 1), jnp.float32)
    ranks = iota((32, LANES), 0)
    for b in range(chunks // 2):
        hits = hits_ref[:, b * 256 : (b + 1) * 256]
        running = mm(hits, upper2)
        rank = jnp.sum(hits.astype(jnp.float32) * (running + carry), axis=0, keepdims=True) - 1.0
        carry = carry + running[:, 255:256]
        for h in range(2):
            a = 2 * b + h
            same = jnp.broadcast_to(rank[:, h * LANES : (h + 1) * LANES], (32, LANES)).astype(jnp.int32) == ranks
            high = jnp.broadcast_to((c[a : a + 1, :] >> 6).astype(jnp.float32), (32, LANES))
            low = jnp.broadcast_to((c[a : a + 1, :] & 63).astype(jnp.float32), (32, LANES))
            place = slice(a * LANES, (a + 1) * LANES)
            picks_ref[0:32, place] = jnp.where(same, high, 0.0).astype(jnp.bfloat16)
            picks_ref[32:64, place] = jnp.where(same, low, 0.0).astype(jnp.bfloat16)
            picks_ref[64:96, place] = jnp.where(same, 1.0, 0.0).astype(jnp.bfloat16)
    found = lax.dot_general(picks_ref[...], hits_ref[...], (((1,), (1,)), ((), ())), preferred_element_type=jnp.float32)
    filled = found[64:96, :] > 0.5
    slots = found[0:32, :] * 64.0 + found[32:64, :]
    slots = jnp.where(filled, slots.astype(jnp.int32) - BIAS, EMPTY_SLOT)
    empty_ref[...] = jnp.where(filled, 0.0, EMPTY)[:most, :]
    for k in range(0, LANES, 2):
        pair = [jnp.broadcast_to(slots[:most, k + j : k + j + 1], (most, LANES)) for j in range(2)]
        cs_ref[k * most : (k + 2) * most, :] = jnp.concatenate(pair, axis=0).astype(jnp.int16)
    load.wait()
    x = x_ref[...]
    high = x.astype(jnp.bfloat16)
    xcat_ref[:, :LANES] = high
    xcat_ref[:, LANES:] = (x - high.astype(jnp.float32)).astype(jnp.bfloat16)
    wanted = jnp.broadcast_to(count - WINDOW, (WINDOW, LANES)) + iota((WINDOW, LANES), 0)
    wanted = wanted.astype(jnp.int16)
    first = (size_rows // 2 - WINDOW) // LANES
    parts = []
    for a in range(first, chunks):
        parts.append(ones_where(wanted == jnp.broadcast_to(crow_ref[a][None], (WINDOW // 16, 16, LANES)).reshape(WINDOW, LANES)))
    both = mm(jnp.concatenate(parts, axis=1), xcat_ref[first * LANES :, :])
    tail_ref[...] = both[:, :LANES] + both[:, LANES:]


def own_kernel(block, xcat_ref, crow_ref, cs_ref, sums_ref, w_ref):
    chunks = crow_ref.shape[0]

    def step(m, carry):
        base = pl.multiple_of(m * block, block)
        for t in range(block // 16):
            cs = cs_ref[pl.ds(base + t * 16, 16), :]
            for a in range(chunks):
                w_ref[t * 16 : (t + 1) * 16, a * LANES : (a + 1) * LANES] = ones_where(cs - crow_ref[a] < INSIDE)
        both = mm(w_ref[...], xcat_ref[...])
        sums_ref[pl.ds(base, block), :] = both[:, :LANES] + both[:, LANES:]
        return carry

    lax.fori_loop(0, cs_ref.shape[0] // block, step, 0)


def tail_kernel(most, sums_ref, tail_ref, cs_ref, y_ref, sq_ref):
    tail = tail_ref[...]
    high = tail.astype(jnp.bfloat16)
    tailcat = jnp.concatenate([high, (tail - high.astype(jnp.float32)).astype(jnp.bfloat16)], axis=1)
    lanes = iota((most, LANES), 1)
    group = 16
    size = group * most

    def add_tail(j, sq):
        base = pl.multiple_of(j * size, size)
        cs = cs_ref[pl.ds(base, size), :]
        parts = [
            ones_where(cs - (iota((size, LANES), 1) + (a * LANES - WINDOW)).astype(jnp.int16) < INSIDE) for a in range(WINDOW // LANES)
        ]
        both = mm(jnp.concatenate(parts, axis=1), tailcat)
        y = sums_ref[pl.ds(base, size), :] + both[:, :LANES] + both[:, LANES:]
        y_ref[pl.ds(base, size), :] = y
        squares = jnp.sum(y * y, axis=1, keepdims=True)
        for i in range(group):
            sq = jnp.where(lanes == j * group + i, squares[i * most : (i + 1) * most, :], sq)
        return sq

    sq_ref[...] = lax.fori_loop(0, y_ref.shape[0] // size, add_tail, jnp.zeros((most, LANES), jnp.float32))


def norm_kernel(most, y_ref, sq_ref, other_ref, empty_ref, gain_ref, out_ref):
    inverse = 1.0 / jnp.sqrt((sq_ref[...] + other_ref[...]) / F + EPSILON)
    empty = empty_ref[...]
    gain = gain_ref[...]
    for k in range(y_ref.shape[0] // most):
        place = slice(k * most, (k + 1) * most)
        out_ref[place, :] = y_ref[place, :] * gain * inverse[:, k : k + 1] + empty[:, k : k + 1]


def place_kernel(most, got_ref, out_ref, starts_v, starts_s, sem):
    nodes = got_ref.shape[0]
    size = nodes * most
    flags = as_bf16(got_ref[...].reshape(size, LANES) < LIMIT)
    slot = iota((nodes, size), 1)
    first = iota((nodes, size), 0) * most
    member = as_bf16((slot >= first) & (slot < first + most))
    counts = mm(member, flags)
    earlier = as_bf16(iota((nodes, nodes), 1) < iota((nodes, nodes), 0))
    starts = mm(earlier, counts.astype(jnp.bfloat16))
    diagonal = jnp.where(iota((nodes, LANES), 0) == iota((nodes, LANES), 1), starts, 0.0)
    starts_v[...] = jnp.sum(diagonal, axis=0, keepdims=True).astype(jnp.int32)
    copy = pltpu.make_async_copy(starts_v, starts_s, sem)
    copy.start()
    out_ref[...] = jnp.zeros_like(out_ref)
    copy.wait()

    for k in range(nodes):
        block = got_ref[k]
        out_ref[pl.ds(starts_s[0, k], most), :] = jnp.where(block < LIMIT, block, 0.0)


VMEM = pl.BlockSpec(memory_space=pltpu.VMEM)
ANY = pl.BlockSpec(memory_space=pl.ANY)


def local(rows, row_mask, key_bucket, gain):
    size_rows, half = rows.shape
    nodes = lax.axis_size("tm")
    most = 3 * size_rows // (4 * nodes)
    chunks = size_rows // LANES
    slots = nodes * most
    f32, bf16, i16 = jnp.float32, jnp.bfloat16, jnp.int16
    tail, xcat, crow, cs, empty = pl.pallas_call(
        functools.partial(index_kernel, most),
        out_shape=(
            jax.ShapeDtypeStruct((WINDOW, half), f32),
            jax.ShapeDtypeStruct((size_rows, 2 * half), bf16),
            jax.ShapeDtypeStruct((chunks, 16, LANES), i16),
            jax.ShapeDtypeStruct((slots, LANES), i16),
            jax.ShapeDtypeStruct((most, LANES), f32),
        ),
        in_specs=[ANY, VMEM, VMEM],
        out_specs=(VMEM,) * 5,
        scratch_shapes=[
            pltpu.VMEM((size_rows, half), f32),
            pltpu.VMEM((nodes, size_rows), bf16),
            pltpu.VMEM((96, size_rows), bf16),
            pltpu.SemaphoreType.DMA,
        ],
        name="index",
    )(rows, row_mask.reshape(chunks, LANES), key_bucket.reshape(chunks, LANES))
    earlier_tail = lax.ppermute(tail, "tm", [(i, (i + 1) % nodes) for i in range(nodes)])
    block = 384
    sums = pl.pallas_call(
        functools.partial(own_kernel, block),
        out_shape=jax.ShapeDtypeStruct((slots, half), f32),
        in_specs=[VMEM] * 3,
        out_specs=VMEM,
        scratch_shapes=[pltpu.VMEM((block, size_rows), bf16)],
        cost_estimate=pl.CostEstimate(flops=2 * slots * size_rows * 2 * half, bytes_accessed=4 * slots * half, transcendentals=0),
        name="own",
    )(xcat, crow, cs)
    y, sq = pl.pallas_call(
        functools.partial(tail_kernel, most),
        out_shape=(jax.ShapeDtypeStruct((slots, half), f32), jax.ShapeDtypeStruct((most, LANES), f32)),
        in_specs=[VMEM] * 3,
        out_specs=(VMEM,) * 2,
        name="tail",
    )(sums, earlier_tail, cs)
    other = lax.ppermute(sq, "rep", [(0, 1), (1, 0)])
    outgoing = pl.pallas_call(
        functools.partial(norm_kernel, most),
        out_shape=jax.ShapeDtypeStruct((slots, half), f32),
        in_specs=[VMEM] * 5,
        out_specs=VMEM,
        name="norm",
    )(y, sq, other, empty, gain.reshape(1, half))
    got = lax.all_to_all(outgoing.reshape(nodes, most * half), "tm", split_axis=0, concat_axis=0, tiled=True)
    got = got.reshape(nodes, most, half)
    return pl.pallas_call(
        functools.partial(place_kernel, most),
        out_shape=jax.ShapeDtypeStruct((slots, half), f32),
        in_specs=[VMEM],
        out_specs=VMEM,
        scratch_shapes=[pltpu.VMEM((1, LANES), jnp.int32), pltpu.SMEM((1, LANES), jnp.int32), pltpu.SemaphoreType.DMA],
        name="place",
    )(got)


def solution(mesh):
    in_specs = (P("tm", "rep"), P("tm"), P("tm"), P("rep"))
    out_specs = P("tm", "rep")
    return jax.shard_map(local, mesh=mesh, in_specs=in_specs, out_specs=out_specs, check_vma=False)
```

time: 159 us -> 95.8 us (0.60)
  blocking collectives: 7.48 us -> 55.5 us
  local copies, waits for them, and re-layouts: 46.9 us -> 1.3 us
  other arithmetic: 40.4 us -> 0 us
  Pallas kernels: 0 us -> 32.9 us
  waiting for transfers between devices: 25.5 us -> 1.96 us
  starting transfers between devices: 26.1 us -> 3.78 us
  matrix products: 10.8 us -> 0 us
    all_to_all x1, blocking collectives: 7.48 us -> 55.5 us  [local(): lax.all_to_all(outgoing.reshape(nodes, most * half), 'tm', split_axis=0,...]
    pallas_call x0 -> x5, Pallas kernels: none -> 32.9 us  [the longest x1 13.9 us: local(): pl.pallas_call(functools.partial(own_kernel, block), out_shape=jax.ShapeD...]
    gather x2 -> x0, local copies, waits for them, and re-layouts: 26.8 us -> none  [the longest x1 18.7 us: local(): offset = spots - start_list[sender]]
    all_to_all x2 -> x0, starting transfers between devices: 25.3 us -> none  [the longest x1 16.3 us: local(): lax.all_to_all(sideband, 'tm', split_axis=0, concat_axis=0, tiled=True)]
    scatter x1 -> x0, other arithmetic: 20.2 us -> none  [compact_rows(): jnp.zeros((size_rows, width), jnp.float32).at[target]]
    all_to_all x2 -> x0, waiting for transfers between devices: 17.8 us -> none  [the longest x1 17.8 us: local(): lax.all_to_all(outgoing, 'tm', split_axis=0, concat_axis=0, tiled=True)]
    scatter x1 -> x0, local copies, waits for them, and re-layouts: 12.1 us -> none  [fill_slots(): jnp.zeros((slots_total, width), jnp.float32).at[slot]]
    dot_general x3 -> x0, matrix products: 10.8 us -> none  [the longest x1 3.94 us: window_sums(): jnp.einsum('ij,bjf->bif', lower, blocks, precision=lax.Precision.HIGHEST)]
  transfers between devices with their start and end apart: 3 -> 2, of which waited for: 2 -> 2; matrix products, arithmetic and copies ran while one was open for 34% -> 0% of each run, Pallas kernels for 0% -> 15%
where the time goes in v1:
time: 95.8 us; the launch traced here: 95.4 us
  blocking collectives  55.5 us (58%)
  Pallas kernels  32.9 us (34%)
  starting transfers between devices  3.78 us (4%)
  waiting for transfers between devices  1.96 us (2%)
  local copies, waits for them, and re-layouts  1.3 us (1%)
    all_to_all x1, blocking collectives, local(): lax.all_to_all(outgoing.reshape(nodes, most * half), 'tm', split_axis=0,...  55.5 us
    pallas_call x1, Pallas kernels, local(): pl.pallas_call(functools.partial(own_kernel, block), out_shape=jax.ShapeD...  13.9 us
    pallas_call x1, Pallas kernels, local(): pl.pallas_call(functools.partial(tail_kernel, most), out_shape=(jax.Shape...  5.69 us
    pallas_call x1, Pallas kernels, local(): pl.pallas_call(functools.partial(index_kernel, most), out_shape=(jax.Shap...  5.62 us
    pallas_call x1, Pallas kernels, local(): pl.pallas_call(functools.partial(place_kernel, most), out_shape=jax.Shape...  4 us
    pallas_call x1, Pallas kernels, local(): pl.pallas_call(functools.partial(norm_kernel, most), out_shape=jax.ShapeD...  3.68 us
    ppermute x1, starting transfers between devices, local(): lax.ppermute(tail, 'tm', [(i, (i + 1) % nodes) for i in range(nodes)])  2.53 us
  transfers between devices with their start and end apart: 2, of which 2 were waited for; matrix products, arithmetic and copies ran while one was open for 0% of the time, Pallas kernels for 15%

profile of v1, /device:TPU:1, one launch (start us, length us, event | category | flops | bytes accessed | tf_op | source)
XLA Modules:
  0.0 95.4 jit_solution(2834117395277002096)
XLA Ops:
  0.0 5.6 %index.1 = (f32[512,128]{1,0:T(8,128)}, bf16[4096,256]{1,0:T(8,128)(2,1)}, s16[32,16,128]{2,1,0:T(8,128)(2,1)}, s16[3072,128]{1,0:T(8,128)(2,1)}, f32[24,128]{1,0:T(8,128)}) custom-call(f32[4096,128]{1,0:T(8,128)} %rows_ref.1, s32[32,128]{1,0:T(8,128)} %bitcast.7, s32[32,128]{1,0:T(8,128)} %bitcast.8), custom_call_target="tpu_custom_call" | custom-call | tf_op jit(solution)/shard_map/index/pallas_call | solution.py:185
  5.6 2.5 %collective-permute-start = (f32[512,128]{1,0:T(8,128)}, f32[512,128]{1,0:T(8,128)S(1)}, u32[]{:S(2)}, u32[]{:S(2)}) collective-permute-start(f32[512,128]{1,0:T(8,128)} %get-tuple-element.15), channel_id=1, source_target_pairs={{0,2},{2,4},{4,6},{6,8},{8,10},{10,12},{12,14},{14,16},{16,18},{18... | collective-permute-start | bytes 786440 | tf_op jit(solution)/shard_map/ppermute | solution.py:204
  8.2 13.9 %own.1.sums_ref = f32[3072,128]{1,0:T(8,128)} custom-call(bf16[4096,256]{1,0:T(8,128)(2,1)} %get-tuple-element.12.xcat_ref, s16[32,16,128]{2,1,0:T(8,128)(2,1)} %get-tuple-element.13.crow_ref, s16[3072,128]{1,0:T(8,128)(2,1)} %get-tuple-element.14.cs_ref), custom_call_target="tpu_custom_call" | custom-call | flops 6442450944 | bytes 1572864 | tf_op jit(solution)/shard_map/own/pallas_call | solution.py:206
  22.0 0.9 collective-permute-done.tail_ref
  23.0 0.0 copy-start
  23.0 0.7 copy-done
  23.7 5.7 %tail.1 = (f32[3072,128]{1,0:T(8,128)}, f32[24,128]{1,0:T(8,128)}) custom-call(f32[3072,128]{1,0:T(8,128)} %own.1.sums_ref, f32[512,128]{1,0:T(8,128)} %copy-done, s16[3072,128]{1,0:T(8,128)(2,1)} %get-tuple-element.14.cs_ref), custom_call_target="tpu_custom_call" | custom-call | tf_op jit(solution)/shard_map/tail/pallas_call | solution.py:215
  29.4 1.3 %collective-permute-start.1 = (f32[24,128]{1,0:T(8,128)}, f32[24,128]{1,0:T(8,128)S(1)}, u32[]{:S(2)}, u32[]{:S(2)}) collective-permute-start(f32[24,128]{1,0:T(8,128)} %get-tuple-element.17.sq_ref), channel_id=1, source_target_pairs={{0,1},{1,0},{2,3},{3,2},{4,5},{5,4},{6,7},{7,6},{8,9},{9,8},{10,11... | collective-permute-start | bytes 36872 | tf_op jit(solution)/shard_map/ppermute | solution.py:222
  30.6 1.0 %collective-permute-done.1.other_ref = f32[24,128]{1,0:T(8,128)S(1)} collective-permute-done((f32[24,128]{1,0:T(8,128)}, f32[24,128]{1,0:T(8,128)S(1)}, u32[]{:S(2)}, u32[]{:S(2)}) %collective-permute-start.1) | collective-permute-done | bytes 12320 | tf_op jit(solution)/shard_map/ppermute | solution.py:222
  31.6 0.0 copy-start.1
  31.6 0.6 copy-done.1
  32.2 3.7 %norm.1 = f32[3072,128]{1,0:T(8,128)} custom-call(f32[3072,128]{1,0:T(8,128)} %get-tuple-element.16.y_ref, f32[24,128]{1,0:T(8,128)} %get-tuple-element.17.sq_ref, f32[24,128]{1,0:T(8,128)} %copy-done.1, f32[24,128]{1,0:T(8,128)} %get-tuple-element.18.empty_ref, f32[1,128]{1,0:T(1,128)} %bitcast.9), custom_call_target="tpu_custom_call" | custom-call | tf_op jit(solution)/shard_map/norm/pallas_call | solution.py:223
  35.9 55.5 %all_to_all.9 = f32[128,1,3072]{2,1,0:T(1,128)} all-to-all(f32[128,1,3072]{2,1,0:T(1,128)} %bitcast.6), channel_id=1, replica_groups=mesh['tm'=128,'rep'=2] {'tm'}, dimensions={0} | all-to-all | bytes 3145728 | tf_op jit(solution)/shard_map/all_to_all | solution.py:230
  91.4 4.0 %place.1 = f32[3072,128]{1,0:T(8,128)} custom-call(f32[128,24,128]{2,1,0:T(8,128)} %bitcast.5), custom_call_target="tpu_custom_call" | custom-call | tf_op jit(solution)/shard_map/place/pallas_call | solution.py:232
Async XLA Ops:
  5.6 17.3 %collective-permute-start = (f32[512,128]{1,0:T(8,128)}, f32[512,128]{1,0:T(8,128)S(1)}, u32[]{:S(2)}, u32[]{:S(2)}) collective-permute-start(f32[512,128]{1,0:T(8,128)} %get-tuple-element.15), channel_id=1, source_target_pairs={{0,2},{2,4},{4,6},{6,8},{8,10},{10,12},{12,14},{14,16},{16,18},{18... | collective-permute-start | bytes 786440 | tf_op jit(solution)/shard_map/ppermute | solution.py:204
  23.0 0.7 copy-start
  29.4 2.3 %collective-permute-start.1 = (f32[24,128]{1,0:T(8,128)}, f32[24,128]{1,0:T(8,128)S(1)}, u32[]{:S(2)}, u32[]{:S(2)}) collective-permute-start(f32[24,128]{1,0:T(8,128)} %get-tuple-element.17.sq_ref), channel_id=1, source_target_pairs={{0,1},{1,0},{2,3},{3,2},{4,5},{5,4},{6,7},{7,6},{8,9},{9,8},{10,11... | collective-permute-start | bytes 36872 | tf_op jit(solution)/shard_map/ppermute | solution.py:222
  31.6 0.6 copy-start.1

commit v2 on v1

v2 whole, which is shorter than its diff:
```python
import functools

import jax
import jax.numpy as jnp
from jax import lax
from jax.experimental import pallas as pl
from jax.experimental.pallas import tpu as pltpu
from jax.sharding import PartitionSpec as P

F = 256
WINDOW = 512
LANES = 128
EPSILON = 1e-06

BIAS = 32768
INSIDE = WINDOW - BIAS
NOT_LIVE = 16384
EMPTY_SLOT = 16384
EMPTY = 1e9
LIMIT = 1e8


def iota(shape, dim):
    return lax.broadcasted_iota(jnp.int32, shape, dim)


def as_bf16(test):
    return jnp.where(test, jnp.float32(1.0), jnp.float32(0.0)).astype(jnp.bfloat16)


def ones_where(test):
    return jnp.where(test, jnp.bfloat16(1.0), jnp.bfloat16(0.0))


def mm(a, b):
    return jnp.dot(a, b, preferred_element_type=jnp.float32)


def index_kernel(rows_ref, mask_ref, tail_ref, xcat_ref, crow_ref, c_ref, x_ref, m_ref, sems):
    size_rows = rows_ref.shape[0]
    chunks = size_rows // LANES
    load_mask = pltpu.make_async_copy(mask_ref, m_ref, sems.at[0])
    load_rows = pltpu.make_async_copy(rows_ref, x_ref, sems.at[1])
    load_mask.start()
    load_rows.start()
    load_mask.wait()
    mask = m_ref[...]
    mask_bf = mask.astype(jnp.float32).astype(jnp.bfloat16)
    upper = as_bf16(iota((LANES, LANES), 0) <= iota((LANES, LANES), 1))
    within = mm(mask_bf, upper)
    totals = mm(mask_bf, jnp.ones((LANES, LANES), jnp.bfloat16))
    below = as_bf16(iota((chunks, chunks), 1) < iota((chunks, chunks), 0))
    before = mm(below, totals.astype(jnp.bfloat16))
    count = (before + totals)[chunks - 1 : chunks, :].astype(jnp.int32)
    c = jnp.where(mask == 1, (within + before - 1.0).astype(jnp.int32), NOT_LIVE)
    c_ref[...] = c
    rows16 = [jnp.broadcast_to(c[a : a + 1, :], (16, LANES)).astype(jnp.int16) for a in range(chunks)]
    for a in range(chunks):
        crow_ref[a] = rows16[a]
    load_rows.wait()
    x = x_ref[...]
    high = x.astype(jnp.bfloat16)
    xcat_ref[:, :LANES] = high
    xcat_ref[:, LANES:] = (x - high.astype(jnp.float32)).astype(jnp.bfloat16)
    wanted = jnp.broadcast_to(count - WINDOW, (WINDOW, LANES)) + iota((WINDOW, LANES), 0)
    wanted = wanted.astype(jnp.int16)
    first = (size_rows // 2 - WINDOW) // LANES
    parts = []
    for a in range(first, chunks):
        parts.append(ones_where(wanted == jnp.broadcast_to(rows16[a][None], (WINDOW // 16, 16, LANES)).reshape(WINDOW, LANES)))
    both = mm(jnp.concatenate(parts, axis=1), xcat_ref[first * LANES :, :])
    tail_ref[...] = both[:, :LANES] + both[:, LANES:]


def find_slots(most, c_ref, key_ref, cs_ref, empty_ref, hits_ref, picks_ref):
    chunks = c_ref.shape[0]
    c = c_ref[...]
    key = jnp.where(c < NOT_LIVE, key_ref[...], -1)
    buckets = iota((LANES, LANES), 0)
    for a in range(chunks):
        hits_ref[:, a * LANES : (a + 1) * LANES] = as_bf16(jnp.broadcast_to(key[a : a + 1, :], (LANES, LANES)) == buckets)
    upper = as_bf16(iota((256, 256), 0) <= iota((256, 256), 1))
    carry = jnp.zeros((LANES, 1), jnp.float32)
    ranks = iota((32, LANES), 0)
    for b in range(chunks // 2):
        hits = hits_ref[:, b * 256 : (b + 1) * 256]
        running = mm(hits, upper)
        rank = jnp.sum(hits.astype(jnp.float32) * (running + carry), axis=0, keepdims=True) - 1.0
        carry = carry + running[:, 255:256]
        for h in range(2):
            a = 2 * b + h
            same = jnp.broadcast_to(rank[:, h * LANES : (h + 1) * LANES], (32, LANES)).astype(jnp.int32) == ranks
            high = jnp.broadcast_to((c[a : a + 1, :] >> 6).astype(jnp.float32), (32, LANES))
            low = jnp.broadcast_to((c[a : a + 1, :] & 63).astype(jnp.float32), (32, LANES))
            place = slice(a * LANES, (a + 1) * LANES)
            picks_ref[0:32, place] = jnp.where(same, high, 0.0).astype(jnp.bfloat16)
            picks_ref[32:64, place] = jnp.where(same, low, 0.0).astype(jnp.bfloat16)
            picks_ref[64:96, place] = jnp.where(same, 1.0, 0.0).astype(jnp.bfloat16)
    found = lax.dot_general(picks_ref[...], hits_ref[...], (((1,), (1,)), ((), ())), preferred_element_type=jnp.float32)
    filled = found[64:96, :] > 0.5
    slots = found[0:32, :] * 64.0 + found[32:64, :]
    slots = jnp.where(filled, slots.astype(jnp.int32) - BIAS, EMPTY_SLOT)
    empty_ref[...] = jnp.where(filled, 0.0, EMPTY)[:most, :]
    for k in range(0, LANES, 2):
        pair = [jnp.broadcast_to(slots[:most, k + j : k + j + 1], (most, LANES)) for j in range(2)]
        cs_ref[k * most : (k + 2) * most, :] = jnp.concatenate(pair, axis=0).astype(jnp.int16)


def own_kernel(most, block, xcat_ref, crow_ref, c_ref, key_ref, sums_ref, cs_ref, empty_ref, hits_ref, picks_ref):
    chunks = crow_ref.shape[0]
    find_slots(most, c_ref, key_ref, cs_ref, empty_ref, hits_ref, picks_ref)

    def step(m, carry):
        base = pl.multiple_of(m * block, block)
        cs = cs_ref[pl.ds(base, block), :]
        both = None
        for a in range(0, chunks, 2):
            parts = []
            for i in range(2):
                row = jnp.broadcast_to(crow_ref[a + i][None], (block // 16, 16, LANES)).reshape(block, LANES)
                parts.append(ones_where(cs - row < INSIDE))
            part = mm(jnp.concatenate(parts, axis=1), xcat_ref[a * LANES : (a + 2) * LANES, :])
            both = part if both is None else both + part
        sums_ref[pl.ds(base, block), :] = both[:, :LANES] + both[:, LANES:]
        return carry

    lax.fori_loop(0, cs_ref.shape[0] // block, step, 0)


def tail_kernel(most, sums_ref, tail_ref, cs_ref, y_ref, sq_ref):
    tail = tail_ref[...]
    high = tail.astype(jnp.bfloat16)
    tailcat = jnp.concatenate([high, (tail - high.astype(jnp.float32)).astype(jnp.bfloat16)], axis=1)
    lanes = iota((most, LANES), 1)
    group = 32
    size = group * most

    def add_tail(j, sq):
        base = pl.multiple_of(j * size, size)
        cs = cs_ref[pl.ds(base, size), :]
        parts = [
            ones_where(cs - (iota((size, LANES), 1) + (a * LANES - WINDOW)).astype(jnp.int16) < INSIDE) for a in range(WINDOW // LANES)
        ]
        both = mm(jnp.concatenate(parts, axis=1), tailcat)
        y = sums_ref[pl.ds(base, size), :] + both[:, :LANES] + both[:, LANES:]
        y_ref[pl.ds(base, size), :] = y
        squares = jnp.sum(y * y, axis=1, keepdims=True)
        for i in range(group):
            sq = jnp.where(lanes == j * group + i, squares[i * most : (i + 1) * most, :], sq)
        return sq

    sq_ref[...] = lax.fori_loop(0, y_ref.shape[0] // size, add_tail, jnp.zeros((most, LANES), jnp.float32))


def norm_kernel(y_ref, sq_ref, other_ref, empty_ref, gain_ref, out_ref):
    inverse = 1.0 / jnp.sqrt((sq_ref[...] + other_ref[...]) / F + EPSILON)
    empty = empty_ref[...]
    gain = gain_ref[...]
    for k in range(y_ref.shape[0]):
        out_ref[k] = y_ref[k] * gain * inverse[:, k : k + 1] + empty[:, k : k + 1]


def place_kernel(most, got_ref, out_ref, starts_v, starts_s, sem):
    nodes = got_ref.shape[0]
    size = nodes * most
    flags = as_bf16(got_ref[...].reshape(size, LANES) < LIMIT)
    slot = iota((nodes, size), 1)
    first = iota((nodes, size), 0) * most
    member = as_bf16((slot >= first) & (slot < first + most))
    counts = mm(member, flags)
    earlier = as_bf16(iota((nodes, nodes), 1) < iota((nodes, nodes), 0))
    starts = mm(earlier, counts.astype(jnp.bfloat16))
    diagonal = jnp.where(iota((nodes, LANES), 0) == iota((nodes, LANES), 1), starts, 0.0)
    starts_v[...] = jnp.sum(diagonal, axis=0, keepdims=True).astype(jnp.int32)
    copy = pltpu.make_async_copy(starts_v, starts_s, sem)
    copy.start()
    out_ref[...] = jnp.zeros_like(out_ref)
    copy.wait()

    for k in range(nodes):
        block = got_ref[k]
        out_ref[pl.ds(starts_s[0, k], most), :] = jnp.where(block < LIMIT, block, 0.0)


VMEM = pl.BlockSpec(memory_space=pltpu.VMEM)
HBM = pl.BlockSpec(memory_space=pltpu.HBM)


def call(kernel, name, outs, ins, scratch, megabytes, **settings):
    params = {"vmem_limit_bytes": megabytes << 20, **settings.pop("params", {})}
    return pl.pallas_call(
        kernel,
        out_shape=outs,
        in_specs=ins,
        out_specs=jax.tree.map(lambda _: VMEM, outs),
        scratch_shapes=scratch,
        compiler_params=pltpu.CompilerParams(**params),
        name=name,
        **settings,
    )


def local(rows, row_mask, key_bucket, gain):
    size_rows, half = rows.shape
    nodes = lax.axis_size("tm")
    most = 3 * size_rows // (4 * nodes)
    chunks = size_rows // LANES
    slots = nodes * most
    f32, bf16, i16, i32 = jnp.float32, jnp.bfloat16, jnp.int16, jnp.int32
    shape = jax.ShapeDtypeStruct
    dma = pltpu.SemaphoreType.DMA
    tail, xcat, crow, c = call(
        index_kernel,
        "index",
        (
            shape((WINDOW, half), f32),
            shape((size_rows, 2 * half), bf16),
            shape((chunks, 16, LANES), i16),
            shape((chunks, LANES), i32),
        ),
        [HBM, HBM],
        [pltpu.VMEM((size_rows, half), f32), pltpu.VMEM((chunks, LANES), i32), dma((2,))],
        50,
    )(rows, row_mask.reshape(chunks, LANES))
    earlier_tail = lax.ppermute(tail, "tm", [(i, (i + 1) % nodes) for i in range(nodes)])
    sums, cs, empty = call(
        functools.partial(own_kernel, most, 32 * most),
        "own",
        (shape((slots, half), f32), shape((slots, LANES), i16), shape((most, LANES), f32)),
        [VMEM] * 4,
        [
            pltpu.VMEM((nodes, size_rows), bf16),
            pltpu.VMEM((96, size_rows), bf16),
        ],
        24,
        cost_estimate=pl.CostEstimate(flops=2 * slots * size_rows * 2 * half, bytes_accessed=4 * slots * half, transcendentals=0),
    )(xcat, crow, c, key_bucket.reshape(chunks, LANES))
    y, sq = call(
        functools.partial(tail_kernel, most),
        "tail",
        (shape((slots, half), f32), shape((most, LANES), f32)),
        [VMEM] * 3,
        [],
        20,
    )(sums, earlier_tail, cs)
    other = lax.ppermute(sq, "rep", [(0, 1), (1, 0)])
    outgoing = call(
        norm_kernel,
        "norm",
        shape((nodes, most, half), f32),
        [VMEM] * 5,
        [],
        12,
    )(y.reshape(nodes, most, half), sq, other, empty, gain.reshape(1, half))
    got = lax.all_to_all(outgoing.reshape(nodes, most * half), "tm", split_axis=0, concat_axis=0, tiled=True)
    got = got.reshape(nodes, most, half)
    return call(
        functools.partial(place_kernel, most),
        "place",
        shape((slots, half), f32),
        [VMEM],
        [pltpu.VMEM((1, LANES), i32), pltpu.SMEM((1, LANES), i32), dma],
        20,
    )(got)


def solution(mesh):
    in_specs = (P("tm", "rep"), P("tm"), P("tm"), P("rep"))
    out_specs = P("tm", "rep")
    return jax.shard_map(local, mesh=mesh, in_specs=in_specs, out_specs=out_specs, check_vma=False)
```

time: 95.8 us -> 79.3 us (0.83)
  Pallas kernels: 32.9 us -> 17.5 us
  blocking collectives: 55.5 us -> 50.8 us
  waiting for transfers between devices: 1.96 us -> 6.19 us
    pallas_call x5, Pallas kernels: 32.9 us -> 17.5 us  [the longest x1 9.22 us: local(): call(functools.partial(own_kernel, most, 32 * most), 'own', (shape((slots...]
    all_to_all x1, blocking collectives: 55.5 us -> 50.8 us  [local(): lax.all_to_all(outgoing.reshape(nodes, most * half), 'tm', split_axis=0,...]
    ppermute x1, waiting for transfers between devices: 0.92 us -> 5.35 us  [local(): lax.ppermute(tail, 'tm', [(i, (i + 1) % nodes) for i in range(nodes)])]
  transfers between devices with their start and end apart: 2 -> 2, of which waited for: 2 -> 2; matrix products, arithmetic and copies ran while one was open for 0% -> 0% of each run, Pallas kernels for 15% -> 12%
where the time goes in v2:
time: 79.3 us; the launch traced here: 79.1 us
  blocking collectives  50.8 us (64%)
  Pallas kernels  17.5 us (22%)
  waiting for transfers between devices  6.19 us (8%)
  starting transfers between devices  3.87 us (5%)
    all_to_all x1, blocking collectives, local(): lax.all_to_all(outgoing.reshape(nodes, most * half), 'tm', split_axis=0,...  50.8 us
    pallas_call x1, Pallas kernels, local(): call(functools.partial(own_kernel, most, 32 * most), 'own', (shape((slots...  9.22 us
    ppermute x1, waiting for transfers between devices, local(): lax.ppermute(tail, 'tm', [(i, (i + 1) % nodes) for i in range(nodes)])  5.35 us
    pallas_call x1, Pallas kernels, local(): call(index_kernel, 'index', (shape((WINDOW, half), f32), shape((size_rows...  2.76 us
    pallas_call x1, Pallas kernels, local(): call(functools.partial(place_kernel, most), 'place', shape((slots, half),...  2.59 us
    ppermute x1, starting transfers between devices, local(): lax.ppermute(tail, 'tm', [(i, (i + 1) % nodes) for i in range(nodes)])  2.53 us
    pallas_call x1, Pallas kernels, local(): call(functools.partial(tail_kernel, most), 'tail', (shape((slots, half),...  1.88 us
  transfers between devices with their start and end apart: 2, of which 2 were waited for; matrix products, arithmetic and copies ran while one was open for 0% of the time, Pallas kernels for 12%

profile of v2, /device:TPU:1, one launch (start us, length us, event | category | flops | bytes accessed | tf_op | source)
XLA Modules:
  0.0 79.1 jit_solution(11186592723019607278)
XLA Ops:
  0.0 0.0 copy-start
  0.0 0.7 copy-done
  0.7 0.0 copy-start.2
  0.7 2.8 %index.1 = (f32[512,128]{1,0:T(8,128)S(1)}, bf16[4096,256]{1,0:T(8,128)(2,1)S(1)}, s16[32,16,128]{2,1,0:T(8,128)(2,1)S(1)}, s32[32,128]{1,0:T(8,128)S(1)}) custom-call(f32[4096,128]{1,0:T(8,128)} %rows_ref.1, s32[32,128]{1,0:T(8,128)S(1)} %bitcast.9), custom_call_target="tpu_custom_call" | custom-call | tf_op jit(solution)/shard_map/index/pallas_call | solution.py:212
  3.5 2.5 %collective-permute-start = (f32[512,128]{1,0:T(8,128)S(1)}, f32[512,128]{1,0:T(8,128)S(1)}, u32[]{:S(2)}, u32[]{:S(2)}) collective-permute-start(f32[512,128]{1,0:T(8,128)S(1)} %get-tuple-element.18), channel_id=1, source_target_pairs={{0,2},{2,4},{4,6},{6,8},{8,10},{10,12},{12,14},{14,16},{16,18},{18... | collective-permute-start | bytes 786440 | tf_op jit(solution)/shard_map/ppermute | solution.py:225
  6.0 0.0 copy-done.2
  6.0 9.2 %own.1 = (f32[3072,128]{1,0:T(8,128)S(1)}, s16[3072,128]{1,0:T(8,128)(2,1)S(1)}, f32[24,128]{1,0:T(8,128)S(1)}) custom-call(bf16[4096,256]{1,0:T(8,128)(2,1)S(1)} %get-tuple-element.14.xcat_ref, s16[32,16,128]{2,1,0:T(8,128)(2,1)S(1)} %get-tuple-element.15.crow_ref, s32[32,128]{1,0:T(8,128)S(1)} %get-tuple-element.16.c_ref, s32[32,128]{1,0:T(8,128)S(1)} %bitcast.11), custom_call_target="tpu_custom_call" | custom-call | flops 6442450944 | bytes 1572864 | tf_op jit(solution)/shard_map/own/pallas_call | solution.py:226
  15.2 0.0 copy-start.1
  15.3 5.4 %collective-permute-done.tail_ref = f32[512,128]{1,0:T(8,128)S(1)} collective-permute-done((f32[512,128]{1,0:T(8,128)S(1)}, f32[512,128]{1,0:T(8,128)S(1)}, u32[]{:S(2)}, u32[]{:S(2)}) %collective-permute-start) | collective-permute-done | bytes 262176 | tf_op jit(solution)/shard_map/ppermute | solution.py:225
  20.6 1.9 %tail.1 = (f32[3072,128]{1,0:T(8,128)S(1)}, f32[24,128]{1,0:T(8,128)S(1)}) custom-call(f32[3072,128]{1,0:T(8,128)S(1)} %get-tuple-element.17.sums_ref, f32[512,128]{1,0:T(8,128)S(1)} %collective-permute-done.tail_ref, s16[3072,128]{1,0:T(8,128)(2,1)S(1)} %get-tuple-element.19.cs_ref), custom_call_target="tpu_custom_call" | custom-call | tf_op jit(solution)/shard_map/tail/pallas_call | solution.py:238
  22.5 1.3 %collective-permute-start.1 = (f32[24,128]{1,0:T(8,128)S(1)}, f32[24,128]{1,0:T(8,128)S(1)}, u32[]{:S(2)}, u32[]{:S(2)}) collective-permute-start(f32[24,128]{1,0:T(8,128)S(1)} %get-tuple-element.21.sq_ref), channel_id=1, source_target_pairs={{0,1},{1,0},{2,3},{3,2},{4,5},{5,4},{6,7},{7,6},{8,9},{9,8},{10,11... | collective-permute-start | bytes 36872 | tf_op jit(solution)/shard_map/ppermute | solution.py:246
  23.8 0.8 %collective-permute-done.1.other_ref = f32[24,128]{1,0:T(8,128)S(1)} collective-permute-done((f32[24,128]{1,0:T(8,128)S(1)}, f32[24,128]{1,0:T(8,128)S(1)}, u32[]{:S(2)}, u32[]{:S(2)}) %collective-permute-start.1) | collective-permute-done | bytes 12320 | tf_op jit(solution)/shard_map/ppermute | solution.py:246
  24.7 0.0 copy-done.1
  24.7 1.1 %norm.1 = f32[128,24,128]{2,1,0:T(8,128)S(1)} custom-call(f32[128,24,128]{2,1,0:T(8,128)S(1)} %bitcast.8, f32[24,128]{1,0:T(8,128)S(1)} %get-tuple-element.21.sq_ref, f32[24,128]{1,0:T(8,128)S(1)} %collective-permute-done.1.other_ref, f32[24,128]{1,0:T(8,128)S(1)} %get-tuple-element.22.empty_ref, f32[1,128]{1,0:T(1,128)S(1)} %bitcast.10), custom_call_target="tpu_custom_call" | custom-call | tf_op jit(solution)/shard_map/norm/pallas_call | solution.py:247
  25.8 50.8 %all_to_all.9 = f32[128,1,3072]{2,1,0:T(1,128)S(1)} all-to-all(f32[128,1,3072]{2,1,0:T(1,128)S(1)} %bitcast.7), channel_id=1, replica_groups=mesh['tm'=128,'rep'=2] {'tm'}, dimensions={0} | all-to-all | bytes 3145728 | tf_op jit(solution)/shard_map/all_to_all | solution.py:255
  76.5 2.6 %place.1 = f32[3072,128]{1,0:T(8,128)} custom-call(f32[128,24,128]{2,1,0:T(8,128)S(1)} %bitcast.6), custom_call_target="tpu_custom_call" | custom-call | tf_op jit(solution)/shard_map/place/pallas_call | solution.py:257
Async XLA Ops:
  0.0 0.7 copy-start
  0.7 5.3 %copy-start.2 = (s32[4096]{0:T(1024)S(1)}, s32[4096]{0:T(1024)}, u32[]{:S(2)}) copy-start(s32[4096]{0:T(1024)} %param.6) | copy-start | bytes 49156
  3.5 17.1 %collective-permute-start = (f32[512,128]{1,0:T(8,128)S(1)}, f32[512,128]{1,0:T(8,128)S(1)}, u32[]{:S(2)}, u32[]{:S(2)}) collective-permute-start(f32[512,128]{1,0:T(8,128)S(1)} %get-tuple-element.18), channel_id=1, source_target_pairs={{0,2},{2,4},{4,6},{6,8},{8,10},{10,12},{12,14},{14,16},{16,18},{18... | collective-permute-start | bytes 786440 | tf_op jit(solution)/shard_map/ppermute | solution.py:225
  15.2 9.4 %copy-start.1 = (f32[128]{0:T(128)S(1)}, f32[128]{0:T(128)}, u32[]{:S(2)}) copy-start(f32[128]{0:T(128)} %param.7) | copy-start | bytes 1540
  22.5 2.2 %collective-permute-start.1 = (f32[24,128]{1,0:T(8,128)S(1)}, f32[24,128]{1,0:T(8,128)S(1)}, u32[]{:S(2)}, u32[]{:S(2)}) collective-permute-start(f32[24,128]{1,0:T(8,128)S(1)} %get-tuple-element.21.sq_ref), channel_id=1, source_target_pairs={{0,1},{1,0},{2,3},{3,2},{4,5},{5,4},{6,7},{7,6},{8,9},{9,8},{10,11... | collective-permute-start | bytes 36872 | tf_op jit(solution)/shard_map/ppermute | solution.py:246

commit v3 on v2

--- a/solution.py
+++ b/solution.py
@@ -11,6 +11,7 @@
 WINDOW = 512
 LANES = 128
 EPSILON = 1e-06
+MESH = pl.DeviceIdType.MESH
 
 BIAS = 32768
 INSIDE = WINDOW - BIAS
@@ -158,6 +159,44 @@
     gain = gain_ref[...]
     for k in range(y_ref.shape[0]):
         out_ref[k] = y_ref[k] * gain * inverse[:, k : k + 1] + empty[:, k : k + 1]
+
+
+def exchange_kernel(nodes, out_ref, got_ref, send_sem, recv_sem):
+    me, rep = lax.axis_index("tm"), lax.axis_index("rep")
+    barrier = pltpu.get_barrier_semaphore()
+
+    def greet(k, carry):
+        pl.semaphore_signal(barrier, inc=1, device_id=(lax.rem(me + k, nodes), rep), device_id_type=MESH)
+        return carry
+
+    lax.fori_loop(1, nodes, greet, 0)
+    got_ref[me] = out_ref[me]
+    pl.semaphore_wait(barrier, nodes - 1)
+
+    def send(k, carry):
+        to = lax.rem(me + k, nodes)
+        pltpu.make_async_remote_copy(
+            src_ref=out_ref.at[to],
+            dst_ref=got_ref.at[me],
+            send_sem=send_sem,
+            recv_sem=recv_sem,
+            device_id=(to, rep),
+            device_id_type=MESH,
+        ).start()
+        return carry
+
+    lax.fori_loop(1, nodes, send, 0)
+    others = pl.ds(0, nodes - 1)
+    every = pltpu.make_async_remote_copy(
+        src_ref=out_ref.at[others],
+        dst_ref=got_ref.at[others],
+        send_sem=send_sem,
+        recv_sem=recv_sem,
+        device_id=(me, 1 - rep),
+        device_id_type=MESH,
+    )
+    every.wait_send()
+    every.wait_recv()
 
 
 def place_kernel(most, got_ref, out_ref, starts_v, starts_s, sem):
@@ -252,8 +291,15 @@
         [],
         12,
     )(y.reshape(nodes, most, half), sq, other, empty, gain.reshape(1, half))
-    got = lax.all_to_all(outgoing.reshape(nodes, most * half), "tm", split_axis=0, concat_axis=0, tiled=True)
-    got = got.reshape(nodes, most, half)
+    got = call(
+        functools.partial(exchange_kernel, nodes),
+        "exchange",
+        shape((nodes, most, half), f32),
+        [VMEM],
+        [dma, dma],
+        12,
+        params={"collective_id": 0, "has_side_effects": True},
+    )(outgoing)
     return call(
         functools.partial(place_kernel, most),
         "place",

time: 79.3 us -> 70.9 us (0.89)
  blocking collectives: 50.8 us -> 0 us
  Pallas kernels: 17.5 us -> 59.9 us
    all_to_all x1 -> x0, blocking collectives: 50.8 us -> none  [local(): lax.all_to_all(outgoing.reshape(nodes, most * half), 'tm', split_axis=0,...]
    pallas_call x0 -> x1, Pallas kernels: none -> 42.3 us  [local(): call(functools.partial(exchange_kernel, nodes), 'exchange', shape((nodes,...]
  transfers between devices with their start and end apart: 2 -> 2, of which waited for: 2 -> 2; matrix products, arithmetic and copies ran while one was open for 0% -> 0% of each run, Pallas kernels for 12% -> 13%
where the time goes in v3:
time: 70.9 us; the launch traced here: 70.7 us
  Pallas kernels  59.9 us (84%)
  waiting for transfers between devices  6.19 us (9%)
  starting transfers between devices  3.87 us (5%)
  local copies, waits for them, and re-layouts  0.73 us (1%)
    pallas_call x1, Pallas kernels, local(): call(functools.partial(exchange_kernel, nodes), 'exchange', shape((nodes,...  42.3 us
    pallas_call x1, Pallas kernels, local(): call(functools.partial(own_kernel, most, 32 * most), 'own', (shape((slots...  9.22 us
    ppermute x1, waiting for transfers between devices, local(): lax.ppermute(tail, 'tm', [(i, (i + 1) % nodes) for i in range(nodes)])  5.35 us
    pallas_call x1, Pallas kernels, local(): call(index_kernel, 'index', (shape((WINDOW, half), f32), shape((size_rows...  2.76 us
    pallas_call x1, Pallas kernels, local(): call(functools.partial(place_kernel, most), 'place', shape((slots, half),...  2.59 us
    ppermute x1, starting transfers between devices, local(): lax.ppermute(tail, 'tm', [(i, (i + 1) % nodes) for i in range(nodes)])  2.53 us
    pallas_call x1, Pallas kernels, local(): call(functools.partial(tail_kernel, most), 'tail', (shape((slots, half),...  1.88 us
  transfers between devices with their start and end apart: 2, of which 2 were waited for; matrix products, arithmetic and copies ran while one was open for 0% of the time, Pallas kernels for 13%

profile of v3, /device:TPU:1, one launch (start us, length us, event | category | flops | bytes accessed | tf_op | source)
XLA Modules:
  0.0 70.7 jit_solution(13908626937675592802)
XLA Ops:
  0.0 0.0 copy-start
  0.0 0.7 %copy-done = s32[4096]{0:T(1024)S(1)} copy-done((s32[4096]{0:T(1024)S(1)}, s32[4096]{0:T(1024)}, u32[]{:S(2)}) %copy-start) | copy-done | bytes 16408
  0.7 0.0 copy-start.2
  0.7 2.8 %index.1 = (f32[512,128]{1,0:T(8,128)S(1)}, bf16[4096,256]{1,0:T(8,128)(2,1)S(1)}, s16[32,16,128]{2,1,0:T(8,128)(2,1)S(1)}, s32[32,128]{1,0:T(8,128)S(1)}) custom-call(f32[4096,128]{1,0:T(8,128)} %rows_ref.1, s32[32,128]{1,0:T(8,128)S(1)} %bitcast.5), custom_call_target="tpu_custom_call" | custom-call | tf_op jit(solution)/shard_map/index/pallas_call | solution.py:251
  3.5 2.5 %collective-permute-start = (f32[512,128]{1,0:T(8,128)S(1)}, f32[512,128]{1,0:T(8,128)S(1)}, u32[]{:S(2)}, u32[]{:S(2)}) collective-permute-start(f32[512,128]{1,0:T(8,128)S(1)} %get-tuple-element.18), channel_id=1, source_target_pairs={{0,2},{2,4},{4,6},{6,8},{8,10},{10,12},{12,14},{14,16},{16,18},{18... | collective-permute-start | bytes 786440 | tf_op jit(solution)/shard_map/ppermute | solution.py:264
  6.0 0.0 copy-done.2
  6.0 9.2 %own.1 = (f32[3072,128]{1,0:T(8,128)S(1)}, s16[3072,128]{1,0:T(8,128)(2,1)S(1)}, f32[24,128]{1,0:T(8,128)S(1)}) custom-call(bf16[4096,256]{1,0:T(8,128)(2,1)S(1)} %get-tuple-element.14.xcat_ref, s16[32,16,128]{2,1,0:T(8,128)(2,1)S(1)} %get-tuple-element.15.crow_ref, s32[32,128]{1,0:T(8,128)S(1)} %get-tuple-element.16.c_ref, s32[32,128]{1,0:T(8,128)S(1)} %bitcast.7), custom_call_target="tpu_custom_call" | custom-call | flops 6442450944 | bytes 1572864 | tf_op jit(solution)/shard_map/own/pallas_call | solution.py:265
  15.2 0.0 copy-start.1
  15.3 5.4 %collective-permute-done.tail_ref = f32[512,128]{1,0:T(8,128)S(1)} collective-permute-done((f32[512,128]{1,0:T(8,128)S(1)}, f32[512,128]{1,0:T(8,128)S(1)}, u32[]{:S(2)}, u32[]{:S(2)}) %collective-permute-start) | collective-permute-done | bytes 262176 | tf_op jit(solution)/shard_map/ppermute | solution.py:264
  20.6 1.9 %tail.1 = (f32[3072,128]{1,0:T(8,128)S(1)}, f32[24,128]{1,0:T(8,128)S(1)}) custom-call(f32[3072,128]{1,0:T(8,128)S(1)} %get-tuple-element.17.sums_ref, f32[512,128]{1,0:T(8,128)S(1)} %collective-permute-done.tail_ref, s16[3072,128]{1,0:T(8,128)(2,1)S(1)} %get-tuple-element.19.cs_ref), custom_call_target="tpu_custom_call" | custom-call | tf_op jit(solution)/shard_map/tail/pallas_call | solution.py:277
  22.5 1.3 %collective-permute-start.1 = (f32[24,128]{1,0:T(8,128)S(1)}, f32[24,128]{1,0:T(8,128)S(1)}, u32[]{:S(2)}, u32[]{:S(2)}) collective-permute-start(f32[24,128]{1,0:T(8,128)S(1)} %get-tuple-element.21.sq_ref), channel_id=1, source_target_pairs={{0,1},{1,0},{2,3},{3,2},{4,5},{5,4},{6,7},{7,6},{8,9},{9,8},{10,11... | collective-permute-start | bytes 36872 | tf_op jit(solution)/shard_map/ppermute | solution.py:285
  23.8 0.8 %collective-permute-done.1.other_ref = f32[24,128]{1,0:T(8,128)S(1)} collective-permute-done((f32[24,128]{1,0:T(8,128)S(1)}, f32[24,128]{1,0:T(8,128)S(1)}, u32[]{:S(2)}, u32[]{:S(2)}) %collective-permute-start.1) | collective-permute-done | bytes 12320 | tf_op jit(solution)/shard_map/ppermute | solution.py:285
  24.7 0.0 copy-done.1
  24.7 1.1 %norm.1.out_ref = f32[128,24,128]{2,1,0:T(8,128)S(1)} custom-call(f32[128,24,128]{2,1,0:T(8,128)S(1)} %bitcast.4, f32[24,128]{1,0:T(8,128)S(1)} %get-tuple-element.21.sq_ref, f32[24,128]{1,0:T(8,128)S(1)} %collective-permute-done.1.other_ref, f32[24,128]{1,0:T(8,128)S(1)} %get-tuple-element.22.empty_ref, f32[1,128]{1,0:T(1,128)S(1)} %bitcast.6), custom_call_target="tpu_custom_call" | custom-call | tf_op jit(solution)/shard_map/norm/pallas_call | solution.py:286
  25.8 42.3 %exchange.1.got_ref = f32[128,24,128]{2,1,0:T(8,128)S(1)} custom-call(f32[128,24,128]{2,1,0:T(8,128)S(1)} %norm.1.out_ref), custom_call_target="tpu_custom_call" | custom-call | tf_op jit(solution)/shard_map/exchange/pallas_call | solution.py:294
  68.1 2.6 %place.1 = f32[3072,128]{1,0:T(8,128)} custom-call(f32[128,24,128]{2,1,0:T(8,128)S(1)} %exchange.1.got_ref), custom_call_target="tpu_custom_call" | custom-call | tf_op jit(solution)/shard_map/place/pallas_call | solution.py:303
Async XLA Ops:
  0.0 0.7 %copy-start = (s32[4096]{0:T(1024)S(1)}, s32[4096]{0:T(1024)}, u32[]{:S(2)}) copy-start(s32[4096]{0:T(1024)} %param.5) | copy-start | bytes 49156
  0.7 5.3 %copy-start.2 = (s32[4096]{0:T(1024)S(1)}, s32[4096]{0:T(1024)}, u32[]{:S(2)}) copy-start(s32[4096]{0:T(1024)} %param.6) | copy-start | bytes 49156
  3.5 17.1 %collective-permute-start = (f32[512,128]{1,0:T(8,128)S(1)}, f32[512,128]{1,0:T(8,128)S(1)}, u32[]{:S(2)}, u32[]{:S(2)}) collective-permute-start(f32[512,128]{1,0:T(8,128)S(1)} %get-tuple-element.18), channel_id=1, source_target_pairs={{0,2},{2,4},{4,6},{6,8},{8,10},{10,12},{12,14},{14,16},{16,18},{18... | collective-permute-start | bytes 786440 | tf_op jit(solution)/shard_map/ppermute | solution.py:264
  15.2 9.4 %copy-start.1 = (f32[128]{0:T(128)S(1)}, f32[128]{0:T(128)}, u32[]{:S(2)}) copy-start(f32[128]{0:T(128)} %param.7) | copy-start | bytes 1540
  22.5 2.2 %collective-permute-start.1 = (f32[24,128]{1,0:T(8,128)S(1)}, f32[24,128]{1,0:T(8,128)S(1)}, u32[]{:S(2)}, u32[]{:S(2)}) collective-permute-start(f32[24,128]{1,0:T(8,128)S(1)} %get-tuple-element.21.sq_ref), channel_id=1, source_target_pairs={{0,1},{1,0},{2,3},{3,2},{4,5},{5,4},{6,7},{7,6},{8,9},{9,8},{10,11... | collective-permute-start | bytes 36872 | tf_op jit(solution)/shard_map/ppermute | solution.py:285

commit v4 on v3

--- a/solution.py
+++ b/solution.py
@@ -153,23 +153,20 @@
     sq_ref[...] = lax.fori_loop(0, y_ref.shape[0] // size, add_tail, jnp.zeros((most, LANES), jnp.float32))
 
 
-def norm_kernel(y_ref, sq_ref, other_ref, empty_ref, gain_ref, out_ref):
+def exchange_kernel(nodes, most, y_ref, sq_ref, other_ref, empty_ref, gain_ref, got_ref, out_ref, send_sem, recv_sem):
+    me, rep = lax.axis_index("tm"), lax.axis_index("rep")
+    barrier = pltpu.get_barrier_semaphore()
+
+    def greet(k, carry):
+        pl.semaphore_signal(barrier, inc=1, device_id=(lax.rem(me + k, nodes), rep), device_id_type=MESH)
+        return carry
+
+    lax.fori_loop(1, nodes, greet, 0)
     inverse = 1.0 / jnp.sqrt((sq_ref[...] + other_ref[...]) / F + EPSILON)
     empty = empty_ref[...]
     gain = gain_ref[...]
-    for k in range(y_ref.shape[0]):
+    for k in range(nodes):
         out_ref[k] = y_ref[k] * gain * inverse[:, k : k + 1] + empty[:, k : k + 1]
-
-
-def exchange_kernel(nodes, out_ref, got_ref, send_sem, recv_sem):
-    me, rep = lax.axis_index("tm"), lax.axis_index("rep")
-    barrier = pltpu.get_barrier_semaphore()
-
-    def greet(k, carry):
-        pl.semaphore_signal(barrier, inc=1, device_id=(lax.rem(me + k, nodes), rep), device_id_type=MESH)
-        return carry
-
-    lax.fori_loop(1, nodes, greet, 0)
     got_ref[me] = out_ref[me]
     pl.semaphore_wait(barrier, nodes - 1)
 
@@ -260,7 +257,7 @@
         [HBM, HBM],
         [pltpu.VMEM((size_rows, half), f32), pltpu.VMEM((chunks, LANES), i32), dma((2,))],
         50,
-    )(rows, row_mask.reshape(chunks, LANES))
+    )(rows, pltpu.with_memory_space_constraint(row_mask.reshape(chunks, LANES), pltpu.HBM))
     earlier_tail = lax.ppermute(tail, "tm", [(i, (i + 1) % nodes) for i in range(nodes)])
     sums, cs, empty = call(
         functools.partial(own_kernel, most, 32 * most),
@@ -283,23 +280,15 @@
         20,
     )(sums, earlier_tail, cs)
     other = lax.ppermute(sq, "rep", [(0, 1), (1, 0)])
-    outgoing = call(
-        norm_kernel,
-        "norm",
+    got = call(
+        functools.partial(exchange_kernel, nodes, most),
+        "exchange",
         shape((nodes, most, half), f32),
         [VMEM] * 5,
-        [],
-        12,
-    )(y.reshape(nodes, most, half), sq, other, empty, gain.reshape(1, half))
-    got = call(
-        functools.partial(exchange_kernel, nodes),
-        "exchange",
-        shape((nodes, most, half), f32),
-        [VMEM],
-        [dma, dma],
+        [pltpu.VMEM((nodes, most, half), f32), dma, dma],
         12,
         params={"collective_id": 0, "has_side_effects": True},
-    )(outgoing)
+    )(y.reshape(nodes, most, half), sq, other, empty, gain.reshape(1, half))
     return call(
         functools.partial(place_kernel, most),
         "place",

time: 70.9 us -> 68.7 us (0.969)
  Pallas kernels: 59.9 us -> 58.4 us
  local copies, waits for them, and re-layouts: 0.73 us -> 0.01 us
    pallas_call x2 -> x1, Pallas kernels: 43.4 us -> 42 us  [local(): call(functools.partial(exchange_kernel, nodes, most), 'exchange', shape((...]
    unnamed x6 -> x4, local copies, waits for them, and re-layouts: 0.73 us -> 0.01 us
where the time goes in v4:
time: 68.7 us; the launch traced here: 68.6 us
  Pallas kernels  58.4 us (85%)
  waiting for transfers between devices  6.19 us (9%)
  starting transfers between devices  3.87 us (6%)
    pallas_call x1, Pallas kernels, local(): call(functools.partial(exchange_kernel, nodes, most), 'exchange', shape((...  42 us
    pallas_call x1, Pallas kernels, local(): call(functools.partial(own_kernel, most, 32 * most), 'own', (shape((slots...  9.21 us
    ppermute x1, waiting for transfers between devices, local(): lax.ppermute(tail, 'tm', [(i, (i + 1) % nodes) for i in range(nodes)])  5.36 us
    pallas_call x1, Pallas kernels, local(): call(index_kernel, 'index', (shape((WINDOW, half), f32), shape((size_rows...  2.77 us
    pallas_call x1, Pallas kernels, local(): call(functools.partial(place_kernel, most), 'place', shape((slots, half),...  2.59 us
    ppermute x1, starting transfers between devices, local(): lax.ppermute(tail, 'tm', [(i, (i + 1) % nodes) for i in range(nodes)])  2.53 us
    pallas_call x1, Pallas kernels, local(): call(functools.partial(tail_kernel, most), 'tail', (shape((slots, half),...  1.87 us
  transfers between devices with their start and end apart: 2, of which 2 were waited for; matrix products, arithmetic and copies ran while one was open for 0% of the time, Pallas kernels for 13%

profile of v4, /device:TPU:1, one launch (start us, length us, event | category | flops | bytes accessed | tf_op | source)
XLA Modules:
  0.0 68.6 jit_solution(17568563246204929715)
XLA Ops:
  0.0 0.0 copy-start.1
  0.0 2.8 %index.1 = (f32[512,128]{1,0:T(8,128)S(1)}, bf16[4096,256]{1,0:T(8,128)(2,1)S(1)}, s16[32,16,128]{2,1,0:T(8,128)(2,1)S(1)}, s32[32,128]{1,0:T(8,128)S(1)}) custom-call(f32[4096,128]{1,0:T(8,128)} %rows_ref.1, s32[32,128]{1,0:T(8,128)} %bitcast.7), custom_call_target="tpu_custom_call" | custom-call | tf_op jit(solution)/shard_map/index/pallas_call | solution.py:248
  2.8 2.5 %collective-permute-start = (f32[512,128]{1,0:T(8,128)S(1)}, f32[512,128]{1,0:T(8,128)S(1)}, u32[]{:S(2)}, u32[]{:S(2)}) collective-permute-start(f32[512,128]{1,0:T(8,128)S(1)} %get-tuple-element.18), channel_id=1, source_target_pairs={{0,2},{2,4},{4,6},{6,8},{8,10},{10,12},{12,14},{14,16},{16,18},{18... | collective-permute-start | bytes 786440 | tf_op jit(solution)/shard_map/ppermute | solution.py:261
  5.3 0.0 copy-done.1
  5.3 9.2 %own.1 = (f32[3072,128]{1,0:T(8,128)S(1)}, s16[3072,128]{1,0:T(8,128)(2,1)S(1)}, f32[24,128]{1,0:T(8,128)S(1)}) custom-call(bf16[4096,256]{1,0:T(8,128)(2,1)S(1)} %get-tuple-element.14.xcat_ref, s16[32,16,128]{2,1,0:T(8,128)(2,1)S(1)} %get-tuple-element.15.crow_ref, s32[32,128]{1,0:T(8,128)S(1)} %get-tuple-element.16.c_ref, s32[32,128]{1,0:T(8,128)S(1)} %bitcast.6), custom_call_target="tpu_custom_call" | custom-call | flops 6442450944 | bytes 1572864 | tf_op jit(solution)/shard_map/own/pallas_call | solution.py:262
  14.5 0.0 copy-start
  14.5 5.4 %collective-permute-done.tail_ref = f32[512,128]{1,0:T(8,128)S(1)} collective-permute-done((f32[512,128]{1,0:T(8,128)S(1)}, f32[512,128]{1,0:T(8,128)S(1)}, u32[]{:S(2)}, u32[]{:S(2)}) %collective-permute-start) | collective-permute-done | bytes 262176 | tf_op jit(solution)/shard_map/ppermute | solution.py:261
  19.9 1.9 %tail.1 = (f32[3072,128]{1,0:T(8,128)S(1)}, f32[24,128]{1,0:T(8,128)S(1)}) custom-call(f32[3072,128]{1,0:T(8,128)S(1)} %get-tuple-element.17.sums_ref, f32[512,128]{1,0:T(8,128)S(1)} %collective-permute-done.tail_ref, s16[3072,128]{1,0:T(8,128)(2,1)S(1)} %get-tuple-element.19.cs_ref), custom_call_target="tpu_custom_call" | custom-call | tf_op jit(solution)/shard_map/tail/pallas_call | solution.py:274
  21.8 1.3 %collective-permute-start.1 = (f32[24,128]{1,0:T(8,128)S(1)}, f32[24,128]{1,0:T(8,128)S(1)}, u32[]{:S(2)}, u32[]{:S(2)}) collective-permute-start(f32[24,128]{1,0:T(8,128)S(1)} %get-tuple-element.21.sq_ref), channel_id=1, source_target_pairs={{0,1},{1,0},{2,3},{3,2},{4,5},{5,4},{6,7},{7,6},{8,9},{9,8},{10,11... | collective-permute-start | bytes 36872 | tf_op jit(solution)/shard_map/ppermute | solution.py:282
  23.1 0.8 %collective-permute-done.1.other_ref = f32[24,128]{1,0:T(8,128)S(1)} collective-permute-done((f32[24,128]{1,0:T(8,128)S(1)}, f32[24,128]{1,0:T(8,128)S(1)}, u32[]{:S(2)}, u32[]{:S(2)}) %collective-permute-start.1) | collective-permute-done | bytes 12320 | tf_op jit(solution)/shard_map/ppermute | solution.py:282
  24.0 0.0 copy-done
  24.0 42.0 %exchange.1.got_ref = f32[128,24,128]{2,1,0:T(8,128)S(1)} custom-call(f32[128,24,128]{2,1,0:T(8,128)S(1)} %bitcast.4, f32[24,128]{1,0:T(8,128)S(1)} %get-tuple-element.21.sq_ref, f32[24,128]{1,0:T(8,128)S(1)} %collective-permute-done.1.other_ref, f32[24,128]{1,0:T(8,128)S(1)} %get-tuple-element.22.empty_ref, f32[1,128]{1,0:T(1,128)S(1)} %bitcast.5), custom_call_target="tpu_custom_call" | custom-call | tf_op jit(solution)/shard_map/exchange/pallas_call | solution.py:283
  66.0 2.6 %place.1 = f32[3072,128]{1,0:T(8,128)} custom-call(f32[128,24,128]{2,1,0:T(8,128)S(1)} %exchange.1.got_ref), custom_call_target="tpu_custom_call" | custom-call | tf_op jit(solution)/shard_map/place/pallas_call | solution.py:292
Async XLA Ops:
  0.0 5.3 %copy-start.1 = (s32[4096]{0:T(1024)S(1)}, s32[4096]{0:T(1024)}, u32[]{:S(2)}) copy-start(s32[4096]{0:T(1024)} %param.6) | copy-start | bytes 49156
  2.8 17.1 %collective-permute-start = (f32[512,128]{1,0:T(8,128)S(1)}, f32[512,128]{1,0:T(8,128)S(1)}, u32[]{:S(2)}, u32[]{:S(2)}) collective-permute-start(f32[512,128]{1,0:T(8,128)S(1)} %get-tuple-element.18), channel_id=1, source_target_pairs={{0,2},{2,4},{4,6},{6,8},{8,10},{10,12},{12,14},{14,16},{16,18},{18... | collective-permute-start | bytes 786440 | tf_op jit(solution)/shard_map/ppermute | solution.py:261
  14.5 9.4 %copy-start = (f32[128]{0:T(128)S(1)}, f32[128]{0:T(128)}, u32[]{:S(2)}) copy-start(f32[128]{0:T(128)} %param.7) | copy-start | bytes 1540
  21.8 2.2 %collective-permute-start.1 = (f32[24,128]{1,0:T(8,128)S(1)}, f32[24,128]{1,0:T(8,128)S(1)}, u32[]{:S(2)}, u32[]{:S(2)}) collective-permute-start(f32[24,128]{1,0:T(8,128)S(1)} %get-tuple-element.21.sq_ref), channel_id=1, source_target_pairs={{0,1},{1,0},{2,3},{3,2},{4,5},{5,4},{6,7},{7,6},{8,9},{9,8},{10,11... | collective-permute-start | bytes 36872 | tf_op jit(solution)/shard_map/ppermute | solution.py:282

commit v5 on v2

--- a/solution.py
+++ b/solution.py
@@ -11,6 +11,7 @@
 WINDOW = 512
 LANES = 128
 EPSILON = 1e-06
+MESH = pl.DeviceIdType.MESH
 
 BIAS = 32768
 INSIDE = WINDOW - BIAS
@@ -36,15 +37,9 @@
     return jnp.dot(a, b, preferred_element_type=jnp.float32)
 
 
-def index_kernel(rows_ref, mask_ref, tail_ref, xcat_ref, crow_ref, c_ref, x_ref, m_ref, sems):
-    size_rows = rows_ref.shape[0]
+def find_tail(x, mask, tail_ref, xcat_ref, crow_ref, c_ref, wait_rows):
+    size_rows = xcat_ref.shape[0]
     chunks = size_rows // LANES
-    load_mask = pltpu.make_async_copy(mask_ref, m_ref, sems.at[0])
-    load_rows = pltpu.make_async_copy(rows_ref, x_ref, sems.at[1])
-    load_mask.start()
-    load_rows.start()
-    load_mask.wait()
-    mask = m_ref[...]
     mask_bf = mask.astype(jnp.float32).astype(jnp.bfloat16)
     upper = as_bf16(iota((LANES, LANES), 0) <= iota((LANES, LANES), 1))
     within = mm(mask_bf, upper)
@@ -57,11 +52,10 @@
     rows16 = [jnp.broadcast_to(c[a : a + 1, :], (16, LANES)).astype(jnp.int16) for a in range(chunks)]
     for a in range(chunks):
         crow_ref[a] = rows16[a]
-    load_rows.wait()
-    x = x_ref[...]
-    high = x.astype(jnp.bfloat16)
+    wait_rows()
+    high = x[...].astype(jnp.bfloat16)
     xcat_ref[:, :LANES] = high
-    xcat_ref[:, LANES:] = (x - high.astype(jnp.float32)).astype(jnp.bfloat16)
+    xcat_ref[:, LANES:] = (x[...] - high.astype(jnp.float32)).astype(jnp.bfloat16)
     wanted = jnp.broadcast_to(count - WINDOW, (WINDOW, LANES)) + iota((WINDOW, LANES), 0)
     wanted = wanted.astype(jnp.int16)
     first = (size_rows // 2 - WINDOW) // LANES
@@ -72,7 +66,7 @@
     tail_ref[...] = both[:, :LANES] + both[:, LANES:]
 
 
-def find_slots(most, c_ref, key_ref, cs_ref, empty_ref, hits_ref, picks_ref):
+def find_slots(most, group, c_ref, key_ref, cs_ref, empty_ref, hits_ref, picks_ref):
     chunks = c_ref.shape[0]
     c = c_ref[...]
     key = jnp.where(c < NOT_LIVE, key_ref[...], -1)
@@ -100,15 +94,16 @@
     filled = found[64:96, :] > 0.5
     slots = found[0:32, :] * 64.0 + found[32:64, :]
     slots = jnp.where(filled, slots.astype(jnp.int32) - BIAS, EMPTY_SLOT)
-    empty_ref[...] = jnp.where(filled, 0.0, EMPTY)[:most, :]
+    empty = jnp.where(filled, 0.0, EMPTY)[:most, :]
+    for g in range(LANES // group):
+        empty_ref[g] = pltpu.roll(empty, (LANES - g * group) % LANES, 1) if g else empty
     for k in range(0, LANES, 2):
         pair = [jnp.broadcast_to(slots[:most, k + j : k + j + 1], (most, LANES)) for j in range(2)]
         cs_ref[k * most : (k + 2) * most, :] = jnp.concatenate(pair, axis=0).astype(jnp.int16)
 
 
-def own_kernel(most, block, xcat_ref, crow_ref, c_ref, key_ref, sums_ref, cs_ref, empty_ref, hits_ref, picks_ref):
+def own_sums(block, xcat_ref, crow_ref, cs_ref, sums_ref):
     chunks = crow_ref.shape[0]
-    find_slots(most, c_ref, key_ref, cs_ref, empty_ref, hits_ref, picks_ref)
 
     def step(m, carry):
         base = pl.multiple_of(m * block, block)
@@ -127,37 +122,123 @@
     lax.fori_loop(0, cs_ref.shape[0] // block, step, 0)
 
 
-def tail_kernel(most, sums_ref, tail_ref, cs_ref, y_ref, sq_ref):
-    tail = tail_ref[...]
+def whole_kernel(
+    nodes, most, group, rows_ref, mask_ref, keys_ref, gains_ref, got_ref,
+    x_ref, m_ref, key_ref, gain_ref, tail_ref, tailin_ref, xcat_ref, crow_ref, c_ref, hits_ref, picks_ref,
+    cs_ref, empty_ref, sums_ref, y_ref, sq_ref, sqin_ref,
+    load_sems, tail_sems, swap_send, swap_recv, send_sem, recv_sem,
+):
+    me, rep = lax.axis_index("tm"), lax.axis_index("rep")
+    barrier = pltpu.get_barrier_semaphore()
+    loads = [
+        pltpu.make_async_copy(source, target, load_sems.at[i])
+        for i, (source, target) in enumerate(((mask_ref, m_ref), (keys_ref, key_ref), (rows_ref, x_ref), (gains_ref, gain_ref)))
+    ]
+    for load in loads:
+        load.start()
+
+    def greet(k, carry):
+        pl.semaphore_signal(barrier, inc=1, device_id=(lax.rem(me + k, nodes), rep), device_id_type=MESH)
+        return carry
+
+    pl.semaphore_signal(barrier, inc=1, device_id=(me, 1 - rep), device_id_type=MESH)
+    lax.fori_loop(1, nodes, greet, 0)
+    loads[0].wait()
+    find_tail(x_ref, m_ref[...], tail_ref, xcat_ref, crow_ref, c_ref, loads[2].wait)
+    pl.semaphore_wait(barrier, nodes)
+    onward = pltpu.make_async_remote_copy(
+        src_ref=tail_ref,
+        dst_ref=tailin_ref,
+        send_sem=tail_sems.at[0],
+        recv_sem=tail_sems.at[1],
+        device_id=(lax.rem(me + 1, nodes), rep),
+        device_id_type=MESH,
+    )
+    onward.start()
+    loads[1].wait()
+    find_slots(most, group, c_ref, key_ref, cs_ref, empty_ref, hits_ref, picks_ref)
+    own_sums(group * most, xcat_ref, crow_ref, cs_ref, sums_ref)
+    onward.wait()
+
+    tail = tailin_ref[...]
     high = tail.astype(jnp.bfloat16)
     tailcat = jnp.concatenate([high, (tail - high.astype(jnp.float32)).astype(jnp.bfloat16)], axis=1)
     lanes = iota((most, LANES), 1)
-    group = 32
+    loads[3].wait()
+    gain = gain_ref[...]
     size = group * most
-
-    def add_tail(j, sq):
-        base = pl.multiple_of(j * size, size)
+    groups = nodes // group
+
+    def place_of(j):
+        return lax.rem(me // group + j, groups)
+
+    def swap(j):
+        return pltpu.make_async_remote_copy(
+            src_ref=sq_ref.at[j],
+            dst_ref=sqin_ref.at[j],
+            send_sem=swap_send.at[j],
+            recv_sem=swap_recv.at[j],
+            device_id=(me, 1 - rep),
+            device_id_type=MESH,
+        )
+
+    def add_tail(j):
+        g = place_of(j)
+        base = pl.multiple_of(g * size, size)
         cs = cs_ref[pl.ds(base, size), :]
         parts = [
             ones_where(cs - (iota((size, LANES), 1) + (a * LANES - WINDOW)).astype(jnp.int16) < INSIDE) for a in range(WINDOW // LANES)
         ]
         both = mm(jnp.concatenate(parts, axis=1), tailcat)
         y = sums_ref[pl.ds(base, size), :] + both[:, :LANES] + both[:, LANES:]
-        y_ref[pl.ds(base, size), :] = y
+        y_ref[pl.ds(g * group, group)] = y.reshape(group, most, LANES)
         squares = jnp.sum(y * y, axis=1, keepdims=True)
+        sq = jnp.zeros((most, LANES), jnp.float32)
         for i in range(group):
-            sq = jnp.where(lanes == j * group + i, squares[i * most : (i + 1) * most, :], sq)
-        return sq
-
-    sq_ref[...] = lax.fori_loop(0, y_ref.shape[0] // size, add_tail, jnp.zeros((most, LANES), jnp.float32))
-
-
-def norm_kernel(y_ref, sq_ref, other_ref, empty_ref, gain_ref, out_ref):
-    inverse = 1.0 / jnp.sqrt((sq_ref[...] + other_ref[...]) / F + EPSILON)
-    empty = empty_ref[...]
-    gain = gain_ref[...]
-    for k in range(y_ref.shape[0]):
-        out_ref[k] = y_ref[k] * gain * inverse[:, k : k + 1] + empty[:, k : k + 1]
+            sq = jnp.where(lanes == i, squares[i * most : (i + 1) * most, :], sq)
+        sq_ref[j] = sq
+        swap(j).start()
+
+    def finish(j):
+        g = place_of(j)
+        swap(j).wait()
+        inverse = 1.0 / jnp.sqrt((sq_ref[j] + sqin_ref[j]) / F + EPSILON)
+        empty = empty_ref[g]
+        for i in range(group):
+            k = g * group + i
+            y_ref[k] = y_ref[k] * gain * inverse[:, i : i + 1] + empty[:, i : i + 1]
+
+        def send(i, carry):
+            to = g * group + lax.rem(me + 1 + i, group)
+            pltpu.make_async_remote_copy(
+                src_ref=y_ref.at[to],
+                dst_ref=got_ref.at[me],
+                send_sem=send_sem,
+                recv_sem=recv_sem,
+                device_id=(to, rep),
+                device_id_type=MESH,
+            ).start()
+            return carry
+
+        lax.fori_loop(0, group - 1 if j == 0 else group, send, 0)
+
+    add_tail(0)
+    for j in range(1, groups):
+        add_tail(j)
+        finish(j - 1)
+    finish(groups - 1)
+    got_ref[me] = y_ref[me]
+    others = pl.ds(0, nodes - 1)
+    every = pltpu.make_async_remote_copy(
+        src_ref=y_ref.at[others],
+        dst_ref=got_ref.at[others],
+        send_sem=send_sem,
+        recv_sem=recv_sem,
+        device_id=(me, 1 - rep),
+        device_id_type=MESH,
+    )
+    every.wait_send()
+    every.wait_recv()
 
 
 def place_kernel(most, got_ref, out_ref, starts_v, starts_s, sem):
@@ -209,51 +290,47 @@
     f32, bf16, i16, i32 = jnp.float32, jnp.bfloat16, jnp.int16, jnp.int32
     shape = jax.ShapeDtypeStruct
     dma = pltpu.SemaphoreType.DMA
-    tail, xcat, crow, c = call(
-        index_kernel,
-        "index",
-        (
-            shape((WINDOW, half), f32),
-            shape((size_rows, 2 * half), bf16),
-            shape((chunks, 16, LANES), i16),
-            shape((chunks, LANES), i32),
-        ),
-        [HBM, HBM],
-        [pltpu.VMEM((size_rows, half), f32), pltpu.VMEM((chunks, LANES), i32), dma((2,))],
-        50,
-    )(rows, row_mask.reshape(chunks, LANES))
-    earlier_tail = lax.ppermute(tail, "tm", [(i, (i + 1) % nodes) for i in range(nodes)])
-    sums, cs, empty = call(
-        functools.partial(own_kernel, most, 32 * most),
-        "own",
-        (shape((slots, half), f32), shape((slots, LANES), i16), shape((most, LANES), f32)),
-        [VMEM] * 4,
+    group = 32
+    vmem = pltpu.VMEM
+    in_hbm = functools.partial(pltpu.with_memory_space_constraint, memory_space=pltpu.HBM)
+    got = call(
+        functools.partial(whole_kernel, nodes, most, group),
+        "whole",
+        shape((nodes, most, half), f32),
+        [HBM] * 4,
         [
-            pltpu.VMEM((nodes, size_rows), bf16),
-            pltpu.VMEM((96, size_rows), bf16),
+            vmem((size_rows, half), f32),
+            vmem((chunks, LANES), i32),
+            vmem((chunks, LANES), i32),
+            vmem((1, half), f32),
+            vmem((WINDOW, half), f32),
+            vmem((WINDOW, half), f32),
+            vmem((size_rows, 2 * half), bf16),
+            vmem((chunks, 16, LANES), i16),
+            vmem((chunks, LANES), i32),
+            vmem((nodes, size_rows), bf16),
+            vmem((96, size_rows), bf16),
+            vmem((slots, LANES), i16),
+            vmem((nodes // group, most, LANES), f32),
+            vmem((slots, half), f32),
+            vmem((nodes, most, half), f32),
+            vmem((nodes // group, most, LANES), f32),
+            vmem((nodes // group, most, LANES), f32),
+            dma((4,)),
+            dma((2,)),
+            dma((nodes // group,)),
+            dma((nodes // group,)),
+            dma,
+            dma,
         ],
-        24,
-        cost_estimate=pl.CostEstimate(flops=2 * slots * size_rows * 2 * half, bytes_accessed=4 * slots * half, transcendentals=0),
-    )(xcat, crow, c, key_bucket.reshape(chunks, LANES))
-    y, sq = call(
-        functools.partial(tail_kernel, most),
-        "tail",
-        (shape((slots, half), f32), shape((most, LANES), f32)),
-        [VMEM] * 3,
-        [],
-        20,
-    )(sums, earlier_tail, cs)
-    other = lax.ppermute(sq, "rep", [(0, 1), (1, 0)])
-    outgoing = call(
-        norm_kernel,
-        "norm",
-        shape((nodes, most, half), f32),
-        [VMEM] * 5,
-        [],
-        12,
-    )(y.reshape(nodes, most, half), sq, other, empty, gain.reshape(1, half))
-    got = lax.all_to_all(outgoing.reshape(nodes, most * half), "tm", split_axis=0, concat_axis=0, tiled=True)
-    got = got.reshape(nodes, most, half)
+        40,
+        params={"collective_id": 0, "has_side_effects": True},
+    )(
+        in_hbm(rows),
+        in_hbm(row_mask.reshape(chunks, LANES)),
+        in_hbm(key_bucket.reshape(chunks, LANES)),
+        in_hbm(gain.reshape(1, half)),
+    )
     return call(
         functools.partial(place_kernel, most),
         "place",

time: 79.3 us -> 63.5 us (0.80)
  blocking collectives: 50.8 us -> 0 us
  Pallas kernels: 17.5 us -> 63.4 us
  waiting for transfers between devices: 6.19 us -> 0 us
  starting transfers between devices: 3.87 us -> 0 us
    all_to_all x1 -> x0, blocking collectives: 50.8 us -> none  [local(): lax.all_to_all(outgoing.reshape(nodes, most * half), 'tm', split_axis=0,...]
    pallas_call x4 -> x1, Pallas kernels: 14.9 us -> 60.8 us  [local(): call(functools.partial(whole_kernel, nodes, most, group), 'whole', shape(...]
    ppermute x2 -> x0, waiting for transfers between devices: 6.19 us -> none  [the longest x1 5.35 us: local(): lax.ppermute(tail, 'tm', [(i, (i + 1) % nodes) for i in range(nodes)])]
    ppermute x2 -> x0, starting transfers between devices: 3.87 us -> none  [the longest x1 2.53 us: local(): lax.ppermute(tail, 'tm', [(i, (i + 1) % nodes) for i in range(nodes)])]
  transfers between devices with their start and end apart: 2 -> 0, of which waited for: 2 -> 0; matrix products, arithmetic and copies ran while one was open for 0% -> 0% of each run, Pallas kernels for 12% -> 0%
where the time goes in v5:
time: 63.5 us; the launch traced here: 63.4 us
  Pallas kernels  63.4 us (100%)
    pallas_call x1, Pallas kernels, local(): call(functools.partial(whole_kernel, nodes, most, group), 'whole', shape(...  60.8 us
    pallas_call x1, Pallas kernels, local(): call(functools.partial(place_kernel, most), 'place', shape((slots, half),...  2.59 us

profile of v5, /device:TPU:1, one launch (start us, length us, event | category | flops | bytes accessed | tf_op | source)
XLA Modules:
  0.0 63.4 jit_solution(3414193087643485623)
XLA Ops:
  0.0 60.8 %whole.1.got_ref = f32[128,24,128]{2,1,0:T(8,128)S(1)} custom-call(f32[4096,128]{1,0:T(8,128)} %rows_ref.1, s32[32,128]{1,0:T(8,128)} %bitcast.3, s32[32,128]{1,0:T(8,128)} %bitcast.4, f32[1,128]{1,0:T(1,128)} %bitcast.5), custom_call_target="tpu_custom_call" | custom-call | tf_op jit(solution)/shard_map/whole/pallas_call | solution.py:296
  60.8 2.6 %place.1 = f32[3072,128]{1,0:T(8,128)} custom-call(f32[128,24,128]{2,1,0:T(8,128)S(1)} %whole.1.got_ref), custom_call_target="tpu_custom_call" | custom-call | tf_op jit(solution)/shard_map/place/pallas_call | solution.py:334

commit v6 on v5

--- a/solution.py
+++ b/solution.py
@@ -37,7 +37,14 @@
     return jnp.dot(a, b, preferred_element_type=jnp.float32)
 
 
-def find_tail(x, mask, tail_ref, xcat_ref, crow_ref, c_ref, wait_rows):
+def split_rows(x_ref, xcat_ref, rows):
+    x = x_ref[rows, :]
+    high = x.astype(jnp.bfloat16)
+    xcat_ref[rows, :LANES] = high
+    xcat_ref[rows, LANES:] = (x - high.astype(jnp.float32)).astype(jnp.bfloat16)
+
+
+def find_tail(first, x_ref, mask, tail_ref, xcat_ref, crow_ref, c_ref, wait_rows):
     size_rows = xcat_ref.shape[0]
     chunks = size_rows // LANES
     mask_bf = mask.astype(jnp.float32).astype(jnp.bfloat16)
@@ -53,12 +60,9 @@
     for a in range(chunks):
         crow_ref[a] = rows16[a]
     wait_rows()
-    high = x[...].astype(jnp.bfloat16)
-    xcat_ref[:, :LANES] = high
-    xcat_ref[:, LANES:] = (x[...] - high.astype(jnp.float32)).astype(jnp.bfloat16)
+    split_rows(x_ref, xcat_ref, slice(first * LANES, size_rows))
     wanted = jnp.broadcast_to(count - WINDOW, (WINDOW, LANES)) + iota((WINDOW, LANES), 0)
     wanted = wanted.astype(jnp.int16)
-    first = (size_rows // 2 - WINDOW) // LANES
     parts = []
     for a in range(first, chunks):
         parts.append(ones_where(wanted == jnp.broadcast_to(rows16[a][None], (WINDOW // 16, 16, LANES)).reshape(WINDOW, LANES)))
@@ -102,11 +106,11 @@
         cs_ref[k * most : (k + 2) * most, :] = jnp.concatenate(pair, axis=0).astype(jnp.int16)
 
 
-def own_sums(block, xcat_ref, crow_ref, cs_ref, sums_ref):
+def own_sums(block, first_j, last_j, place_of, xcat_ref, crow_ref, cs_ref, sums_ref):
     chunks = crow_ref.shape[0]
 
-    def step(m, carry):
-        base = pl.multiple_of(m * block, block)
+    def step(j, carry):
+        base = pl.multiple_of(place_of(j) * block, block)
         cs = cs_ref[pl.ds(base, block), :]
         both = None
         for a in range(0, chunks, 2):
@@ -119,7 +123,7 @@
         sums_ref[pl.ds(base, block), :] = both[:, :LANES] + both[:, LANES:]
         return carry
 
-    lax.fori_loop(0, cs_ref.shape[0] // block, step, 0)
+    lax.fori_loop(first_j, last_j, step, 0)
 
 
 def whole_kernel(
@@ -130,10 +134,17 @@
 ):
     me, rep = lax.axis_index("tm"), lax.axis_index("rep")
     barrier = pltpu.get_barrier_semaphore()
-    loads = [
-        pltpu.make_async_copy(source, target, load_sems.at[i])
-        for i, (source, target) in enumerate(((mask_ref, m_ref), (keys_ref, key_ref), (rows_ref, x_ref), (gains_ref, gain_ref)))
-    ]
+    size_rows = x_ref.shape[0]
+    first = (size_rows // 2 - WINDOW) // LANES
+    early, late = slice(0, first * LANES), slice(first * LANES, size_rows)
+    pairs = (
+        (mask_ref, m_ref),
+        (rows_ref.at[late, :], x_ref.at[late, :]),
+        (keys_ref, key_ref),
+        (rows_ref.at[early, :], x_ref.at[early, :]),
+        (gains_ref, gain_ref),
+    )
+    loads = [pltpu.make_async_copy(source, target, load_sems.at[i]) for i, (source, target) in enumerate(pairs)]
     for load in loads:
         load.start()
 
@@ -144,7 +155,7 @@
     pl.semaphore_signal(barrier, inc=1, device_id=(me, 1 - rep), device_id_type=MESH)
     lax.fori_loop(1, nodes, greet, 0)
     loads[0].wait()
-    find_tail(x_ref, m_ref[...], tail_ref, xcat_ref, crow_ref, c_ref, loads[2].wait)
+    find_tail(first, x_ref, m_ref[...], tail_ref, xcat_ref, crow_ref, c_ref, loads[1].wait)
     pl.semaphore_wait(barrier, nodes)
     onward = pltpu.make_async_remote_copy(
         src_ref=tail_ref,
@@ -155,22 +166,28 @@
         device_id_type=MESH,
     )
     onward.start()
-    loads[1].wait()
+    loads[2].wait()
     find_slots(most, group, c_ref, key_ref, cs_ref, empty_ref, hits_ref, picks_ref)
-    own_sums(group * most, xcat_ref, crow_ref, cs_ref, sums_ref)
+    loads[3].wait()
+    split_rows(x_ref, xcat_ref, early)
+    size = group * most
+    groups = nodes // group
+
+    def place_of(j):
+        return lax.rem(me // group + j, groups)
+
+    def own(first_j, last_j):
+        own_sums(size, first_j, last_j, place_of, xcat_ref, crow_ref, cs_ref, sums_ref)
+
+    own(0, groups - 1)
     onward.wait()
 
     tail = tailin_ref[...]
     high = tail.astype(jnp.bfloat16)
     tailcat = jnp.concatenate([high, (tail - high.astype(jnp.float32)).astype(jnp.bfloat16)], axis=1)
     lanes = iota((most, LANES), 1)
-    loads[3].wait()
+    loads[4].wait()
     gain = gain_ref[...]
-    size = group * most
-    groups = nodes // group
-
-    def place_of(j):
-        return lax.rem(me // group + j, groups)
 
     def swap(j):
         return pltpu.make_async_remote_copy(
@@ -223,9 +240,12 @@
         lax.fori_loop(0, group - 1 if j == 0 else group, send, 0)
 
     add_tail(0)
-    for j in range(1, groups):
+    for j in range(1, groups - 1):
         add_tail(j)
         finish(j - 1)
+    own(groups - 1, groups)
+    finish(groups - 2)
+    add_tail(groups - 1)
     finish(groups - 1)
     got_ref[me] = y_ref[me]
     others = pl.ds(0, nodes - 1)
@@ -316,7 +336,7 @@
             vmem((nodes, most, half), f32),
             vmem((nodes // group, most, LANES), f32),
             vmem((nodes // group, most, LANES), f32),
-            dma((4,)),
+            dma((5,)),
             dma((2,)),
             dma((nodes // group,)),
             dma((nodes // group,)),

time: 63.5 us -> 62.2 us (0.980)
  Pallas kernels: 63.4 us -> 62.1 us
    pallas_call x1, Pallas kernels: 60.8 us -> 59.5 us  [local(): call(functools.partial(whole_kernel, nodes, most, group), 'whole', shape(...]
where the time goes in v6:
time: 62.2 us; the launch traced here: 62.1 us
  Pallas kernels  62.1 us (100%)
    pallas_call x1, Pallas kernels, local(): call(functools.partial(whole_kernel, nodes, most, group), 'whole', shape(...  59.5 us
    pallas_call x1, Pallas kernels, local(): call(functools.partial(place_kernel, most), 'place', shape((slots, half),...  2.59 us

profile of v6, /device:TPU:1, one launch (start us, length us, event | category | flops | bytes accessed | tf_op | source)
XLA Modules:
  0.0 62.1 jit_solution(13505165855214316691)
XLA Ops:
  0.0 59.5 %whole.1.got_ref = f32[128,24,128]{2,1,0:T(8,128)S(1)} custom-call(f32[4096,128]{1,0:T(8,128)} %rows_ref.1, s32[32,128]{1,0:T(8,128)} %bitcast.3, s32[32,128]{1,0:T(8,128)} %bitcast.4, f32[1,128]{1,0:T(1,128)} %bitcast.5), custom_call_target="tpu_custom_call" | custom-call | tf_op jit(solution)/shard_map/whole/pallas_call | solution.py:316
  59.5 2.6 %place.1 = f32[3072,128]{1,0:T(8,128)} custom-call(f32[128,24,128]{2,1,0:T(8,128)S(1)} %whole.1.got_ref), custom_call_target="tpu_custom_call" | custom-call | tf_op jit(solution)/shard_map/place/pallas_call | solution.py:354

commit v7 on v6

--- a/solution.py
+++ b/solution.py
@@ -11,6 +11,7 @@
 WINDOW = 512
 LANES = 128
 EPSILON = 1e-06
+TAIL_PARTS = 2
 MESH = pl.DeviceIdType.MESH
 
 BIAS = 32768
@@ -61,13 +62,18 @@
         crow_ref[a] = rows16[a]
     wait_rows()
     split_rows(x_ref, xcat_ref, slice(first * LANES, size_rows))
-    wanted = jnp.broadcast_to(count - WINDOW, (WINDOW, LANES)) + iota((WINDOW, LANES), 0)
-    wanted = wanted.astype(jnp.int16)
-    parts = []
-    for a in range(first, chunks):
-        parts.append(ones_where(wanted == jnp.broadcast_to(rows16[a][None], (WINDOW // 16, 16, LANES)).reshape(WINDOW, LANES)))
-    both = mm(jnp.concatenate(parts, axis=1), xcat_ref[first * LANES :, :])
-    tail_ref[...] = both[:, :LANES] + both[:, LANES:]
+    size = WINDOW // TAIL_PARTS
+
+    def part(h):
+        wanted = jnp.broadcast_to(count - WINDOW + h * size, (size, LANES)) + iota((size, LANES), 0)
+        wanted = wanted.astype(jnp.int16)
+        parts = []
+        for a in range(first, chunks):
+            parts.append(ones_where(wanted == jnp.broadcast_to(rows16[a][None], (size // 16, 16, LANES)).reshape(size, LANES)))
+        both = mm(jnp.concatenate(parts, axis=1), xcat_ref[first * LANES :, :])
+        tail_ref[h] = both[:, :LANES] + both[:, LANES:]
+
+    return part
 
 
 def find_slots(most, group, c_ref, key_ref, cs_ref, empty_ref, hits_ref, picks_ref):
@@ -130,7 +136,7 @@
     nodes, most, group, rows_ref, mask_ref, keys_ref, gains_ref, got_ref,
     x_ref, m_ref, key_ref, gain_ref, tail_ref, tailin_ref, xcat_ref, crow_ref, c_ref, hits_ref, picks_ref,
     cs_ref, empty_ref, sums_ref, y_ref, sq_ref, sqin_ref,
-    load_sems, tail_sems, swap_send, swap_recv, send_sem, recv_sem,
+    load_sems, tail_send, tail_recv, swap_send, swap_recv, send_sem, recv_sem,
 ):
     me, rep = lax.axis_index("tm"), lax.axis_index("rep")
     barrier = pltpu.get_barrier_semaphore()
@@ -145,8 +151,8 @@
         (gains_ref, gain_ref),
     )
     loads = [pltpu.make_async_copy(source, target, load_sems.at[i]) for i, (source, target) in enumerate(pairs)]
-    for load in loads:
-        load.start()
+    for i in (0, 1, 2, 4):
+        loads[i].start()
 
     def greet(k, carry):
         pl.semaphore_signal(barrier, inc=1, device_id=(lax.rem(me + k, nodes), rep), device_id_type=MESH)
@@ -155,18 +161,26 @@
     pl.semaphore_signal(barrier, inc=1, device_id=(me, 1 - rep), device_id_type=MESH)
     lax.fori_loop(1, nodes, greet, 0)
     loads[0].wait()
-    find_tail(first, x_ref, m_ref[...], tail_ref, xcat_ref, crow_ref, c_ref, loads[1].wait)
-    pl.semaphore_wait(barrier, nodes)
-    onward = pltpu.make_async_remote_copy(
-        src_ref=tail_ref,
-        dst_ref=tailin_ref,
-        send_sem=tail_sems.at[0],
-        recv_sem=tail_sems.at[1],
-        device_id=(lax.rem(me + 1, nodes), rep),
-        device_id_type=MESH,
-    )
-    onward.start()
-    loads[2].wait()
+    tail_part = find_tail(first, x_ref, m_ref[...], tail_ref, xcat_ref, crow_ref, c_ref, loads[1].wait)
+
+    def onward(h):
+        return pltpu.make_async_remote_copy(
+            src_ref=tail_ref.at[h],
+            dst_ref=tailin_ref.at[h],
+            send_sem=tail_send.at[h],
+            recv_sem=tail_recv.at[h],
+            device_id=(lax.rem(me + 1, nodes), rep),
+            device_id_type=MESH,
+        )
+
+    for h in range(TAIL_PARTS):
+        tail_part(h)
+        if h == 0:
+            pl.semaphore_wait(barrier, nodes)
+        if h == TAIL_PARTS - 1:
+            loads[3].start()
+            loads[2].wait()
+        onward(h).start()
     find_slots(most, group, c_ref, key_ref, cs_ref, empty_ref, hits_ref, picks_ref)
     loads[3].wait()
     split_rows(x_ref, xcat_ref, early)
@@ -180,9 +194,10 @@
         own_sums(size, first_j, last_j, place_of, xcat_ref, crow_ref, cs_ref, sums_ref)
 
     own(0, groups - 1)
-    onward.wait()
-
-    tail = tailin_ref[...]
+    for h in range(TAIL_PARTS):
+        onward(h).wait()
+
+    tail = tailin_ref[...].reshape(WINDOW, LANES)
     high = tail.astype(jnp.bfloat16)
     tailcat = jnp.concatenate([high, (tail - high.astype(jnp.float32)).astype(jnp.bfloat16)], axis=1)
     lanes = iota((most, LANES), 1)
@@ -263,12 +278,7 @@
 
 def place_kernel(most, got_ref, out_ref, starts_v, starts_s, sem):
     nodes = got_ref.shape[0]
-    size = nodes * most
-    flags = as_bf16(got_ref[...].reshape(size, LANES) < LIMIT)
-    slot = iota((nodes, size), 1)
-    first = iota((nodes, size), 0) * most
-    member = as_bf16((slot >= first) & (slot < first + most))
-    counts = mm(member, flags)
+    counts = jnp.sum(jnp.where(got_ref[...] < LIMIT, 1.0, 0.0), axis=1)
     earlier = as_bf16(iota((nodes, nodes), 1) < iota((nodes, nodes), 0))
     starts = mm(earlier, counts.astype(jnp.bfloat16))
     diagonal = jnp.where(iota((nodes, LANES), 0) == iota((nodes, LANES), 1), starts, 0.0)
@@ -323,8 +333,8 @@
             vmem((chunks, LANES), i32),
             vmem((chunks, LANES), i32),
             vmem((1, half), f32),
-            vmem((WINDOW, half), f32),
-            vmem((WINDOW, half), f32),
+            vmem((TAIL_PARTS, WINDOW // TAIL_PARTS, half), f32),
+            vmem((TAIL_PARTS, WINDOW // TAIL_PARTS, half), f32),
             vmem((size_rows, 2 * half), bf16),
             vmem((chunks, 16, LANES), i16),
             vmem((chunks, LANES), i32),
@@ -337,7 +347,8 @@
             vmem((nodes // group, most, LANES), f32),
             vmem((nodes // group, most, LANES), f32),
             dma((5,)),
-            dma((2,)),
+            dma((TAIL_PARTS,)),
+            dma((TAIL_PARTS,)),
             dma((nodes // group,)),
             dma((nodes // group,)),
             dma,

time: 62.2 us -> 62.4 us (level)
  no operation moved by 1% of the time
where the time goes in v7:
time: 62.4 us
  Pallas kernels  62.4 us (100%)
    pallas_call x1, Pallas kernels, local(): call(functools.partial(whole_kernel, nodes, most, group), 'whole', shape(...  60 us
    pallas_call x1, Pallas kernels, local(): call(functools.partial(place_kernel, most), 'place', shape((slots, half),...  2.39 us

profile of v7, /device:TPU:1, one launch (start us, length us, event | category | flops | bytes accessed | tf_op | source)
XLA Modules:
  0.0 62.4 jit_solution(4222030251873348180)
XLA Ops:
  0.0 60.0 %whole.1.got_ref = f32[128,24,128]{2,1,0:T(8,128)S(1)} custom-call(f32[4096,128]{1,0:T(8,128)} %rows_ref.1, s32[32,128]{1,0:T(8,128)} %bitcast.3, s32[32,128]{1,0:T(8,128)} %bitcast.4, f32[1,128]{1,0:T(1,128)} %bitcast.5), custom_call_target="tpu_custom_call" | custom-call | tf_op jit(solution)/shard_map/whole/pallas_call | solution.py:326
  60.0 2.4 %place.1 = f32[3072,128]{1,0:T(8,128)} custom-call(f32[128,24,128]{2,1,0:T(8,128)S(1)} %whole.1.got_ref), custom_call_target="tpu_custom_call" | custom-call | tf_op jit(solution)/shard_map/place/pallas_call | solution.py:365

commit v8 on v7

--- a/solution.py
+++ b/solution.py
@@ -11,7 +11,7 @@
 WINDOW = 512
 LANES = 128
 EPSILON = 1e-06
-TAIL_PARTS = 2
+TAIL_PARTS = 1
 MESH = pl.DeviceIdType.MESH
 
 BIAS = 32768

time: 62.4 us -> 62 us (level)
  no operation moved by 1% of the time
where the time goes in v8:
time: 62 us; the launch traced here: 61.9 us
  Pallas kernels  61.9 us (100%)
    pallas_call x1, Pallas kernels, local(): call(functools.partial(whole_kernel, nodes, most, group), 'whole', shape(...  59.5 us
    pallas_call x1, Pallas kernels, local(): call(functools.partial(place_kernel, most), 'place', shape((slots, half),...  2.39 us

profile of v8, /device:TPU:1, one launch (start us, length us, event | category | flops | bytes accessed | tf_op | source)
XLA Modules:
  0.0 61.9 jit_solution(13604331895512319811)
XLA Ops:
  0.0 59.5 %whole.1.got_ref = f32[128,24,128]{2,1,0:T(8,128)S(1)} custom-call(f32[4096,128]{1,0:T(8,128)} %rows_ref.1, s32[32,128]{1,0:T(8,128)} %bitcast.3, s32[32,128]{1,0:T(8,128)} %bitcast.4, f32[1,128]{1,0:T(1,128)} %bitcast.5), custom_call_target="tpu_custom_call" | custom-call | tf_op jit(solution)/shard_map/whole/pallas_call | solution.py:326
  59.5 2.4 %place.1 = f32[3072,128]{1,0:T(8,128)} custom-call(f32[128,24,128]{2,1,0:T(8,128)S(1)} %whole.1.got_ref), custom_call_target="tpu_custom_call" | custom-call | tf_op jit(solution)/shard_map/place/pallas_call | solution.py:365

commit v9 on v8

--- a/solution.py
+++ b/solution.py
@@ -258,8 +258,8 @@
     for j in range(1, groups - 1):
         add_tail(j)
         finish(j - 1)
+    finish(groups - 2)
     own(groups - 1, groups)
-    finish(groups - 2)
     add_tail(groups - 1)
     finish(groups - 1)
     got_ref[me] = y_ref[me]

time: 62 us -> 62 us (level)
  no operation moved by 1% of the time
where the time goes in v9:
time: 62 us; the launch traced here: 61.9 us
  Pallas kernels  61.9 us (100%)
    pallas_call x1, Pallas kernels, local(): call(functools.partial(whole_kernel, nodes, most, group), 'whole', shape(...  59.5 us
    pallas_call x1, Pallas kernels, local(): call(functools.partial(place_kernel, most), 'place', shape((slots, half),...  2.39 us

profile of v9, /device:TPU:1, one launch (start us, length us, event | category | flops | bytes accessed | tf_op | source)
XLA Modules:
  0.0 61.9 jit_solution(14216574057359875766)
XLA Ops:
  0.0 59.5 %whole.1.got_ref = f32[128,24,128]{2,1,0:T(8,128)S(1)} custom-call(f32[4096,128]{1,0:T(8,128)} %rows_ref.1, s32[32,128]{1,0:T(8,128)} %bitcast.3, s32[32,128]{1,0:T(8,128)} %bitcast.4, f32[1,128]{1,0:T(1,128)} %bitcast.5), custom_call_target="tpu_custom_call" | custom-call | tf_op jit(solution)/shard_map/whole/pallas_call | solution.py:326
  59.5 2.4 %place.1 = f32[3072,128]{1,0:T(8,128)} custom-call(f32[128,24,128]{2,1,0:T(8,128)S(1)} %whole.1.got_ref), custom_call_target="tpu_custom_call" | custom-call | tf_op jit(solution)/shard_map/place/pallas_call | solution.py:365
